TPU v7x, 128 devices: a whole 4x4x4 slice. The times are simulated.
128 devices in a mesh: gx: 8 (over z, core), gy: 16 (over y, x).
Axes of the slice: x: 4, y: 4, z: 4, core: 2. Of those that a mesh axis runs over, the one named last changes fastest.
Arguments:
- matrix_rows: float32 [16384, 1024], P(('gx', 'gy')), may hold values from -1.1 to 1.1
- tile_owner: int32 [2080], replicated, may hold values from 0 to 127, as said below
- tile_slot: int32 [2080], replicated, may hold values from 0 to 16, as said below
Outputs:
- packed_tiles: float32 [2176, 256, 256], P(('gx', 'gy'))
Inputs may be any that keep to these rules, and one draw needn't show every extreme that they name: `tile_owner`: give tile (I, J) the class (c, r) as follows, with a = I // 8, b = J // 8, i = I % 8, j = J % 8: if a == b, c = a and r = i when i - j < 4, else r = j; if a > b and (a - b > 4, or a - b == 4 with i + j even), c = b and r = i; otherwise c = a and r = j. The owner of a class (c, r) tile is one of the devices c * 16 to c * 16 + 15. Every owner holds 16 or 17 tiles. At most 3 tiles of one class share an owner, and in every draw some owner holds exactly 3 tiles of one class. `tile_slot`: the tiles of one owner take the slots 0 to their count - 1, each once.
All inputs are finite; a program needn't handle non-finite values.
Results may differ from a plain program's by a relative error of at most 0.0003.
Values sent between devices are 32-bit elements; how exact they have to be, the bound alone decides.
A program may use at most 128 MiB of HBM per device.

v0:
```python
import jax
import jax.numpy as jnp
import numpy as np
from jax import lax
from jax.sharding import PartitionSpec as P


def from_behind(value, axis, steps):
    count = lax.axis_size(axis)
    pairs = [(source, (source + steps) % count) for source in range(count)]
    return lax.ppermute(value, axis, pairs)


def classify(row_tile, col_tile, half_tiles, count_x):
    group_a = row_tile // half_tiles
    group_b = col_tile // half_tiles
    inner_i = row_tile % half_tiles
    inner_j = col_tile % half_tiles
    same = group_a == group_b
    within_row = inner_i - inner_j < half_tiles // 2
    gap = group_a - group_b
    across_row = jnp.logical_or(
        gap > count_x // 2, jnp.logical_and(gap == count_x // 2, (inner_i + inner_j) % 2 == 0)
    )
    rowwise = jnp.where(same, within_row, across_row)
    class_r = jnp.where(rowwise, inner_i, inner_j)
    return (class_r, rowwise)


def per_device(matrix_rows, tile_owner, tile_slot):
    rows_dev, width = matrix_rows.shape
    tile_size = 2 * rows_dev
    count_x = lax.axis_size("gx")
    count_y = lax.axis_size("gy")
    half_tiles = count_y // 2
    half_x = count_x // 2
    capacity = count_x // 4 + 1
    devices = count_x * count_y
    tile_count = devices // 2
    lower_count = tile_owner.shape[0]
    slot_count = (lower_count + devices - 1) // devices
    x_index = lax.axis_index("gx")
    y_index = lax.axis_index("gy")
    own_r = y_index // 2
    own_h = y_index % 2
    shifted = [matrix_rows]
    for step in range(1, half_x + 1):
        shifted.append(from_behind(matrix_rows, "gx", step))
    first_count = half_tiles // 2 + 1
    offsets = jnp.arange(first_count, dtype=jnp.int32)
    first_cols = (own_r - offsets) % half_tiles
    first_valid = jnp.logical_or(offsets < half_tiles // 2, own_r < half_tiles // 2)
    flag = (x_index >= half_x).astype(jnp.int32)
    last_cols = 2 * jnp.arange(half_tiles // 2, dtype=jnp.int32) + (own_r + flag) % 2
    middle = half_x - 1
    middle_cols = jnp.tile(jnp.arange(half_tiles, dtype=jnp.int32), middle)
    col_of = jnp.concatenate([first_cols, middle_cols, last_cols])
    valid = jnp.concatenate([first_valid, jnp.ones((middle * half_tiles + half_tiles // 2,), bool)])
    step_table = np.concatenate(
        [
            np.zeros(first_count, np.int32),
            np.repeat(np.arange(1, half_x, dtype=np.int32), half_tiles),
            np.full(half_tiles // 2, half_x, np.int32),
        ]
    )
    step_of = jnp.asarray(step_table, jnp.int32)
    stacked = jnp.stack(shifted)
    full = jnp.einsum(
        "srk,ck->src",
        stacked,
        lax.all_gather(matrix_rows, "gy", axis=0, tiled=True),
        precision=lax.Precision.HIGHEST,
        preferred_element_type=jnp.float32,
    )
    full = full.reshape(half_x + 1, rows_dev, half_tiles, tile_size)
    pieces = full[step_of, :, col_of, :]
    source_x = (x_index - step_of) % count_x
    rowwise = jnp.where(step_of == 0, col_of <= own_r, source_x > x_index)
    row_tile = jnp.where(rowwise, source_x * half_tiles + own_r, x_index * half_tiles + col_of)
    col_tile = jnp.where(rowwise, x_index * half_tiles + col_of, source_x * half_tiles + own_r)
    row_inside = own_h * rows_dev + lax.broadcasted_iota(jnp.int32, (rows_dev, tile_size), 0)
    col_inside = lax.broadcasted_iota(jnp.int32, (rows_dev, tile_size), 1)
    above = jnp.logical_and((row_tile == col_tile)[:, None, None], (row_inside < col_inside)[None])
    pieces = jnp.where(above, jnp.float32(0.0), pieces)
    tile_index = jnp.where(valid, row_tile * (row_tile + 1) // 2 + col_tile, 0)
    target = jnp.where(valid, tile_owner[tile_index] % count_y, count_y)
    earlier = jnp.logical_and(
        target[:, None] == target[None, :], tile_index[None, :] < tile_index[:, None]
    )
    earlier = jnp.logical_and(earlier, valid[None, :])
    rank = jnp.sum(earlier.astype(jnp.int32), axis=1)
    outgoing = jnp.zeros((count_y, capacity, rows_dev, tile_size), jnp.float32)
    outgoing = outgoing.at[target, rank].set(pieces, mode="drop")
    incoming = lax.all_to_all(outgoing, "gy", split_axis=0, concat_axis=0, tiled=True)
    my_index = x_index * count_y + y_index
    inverse = jnp.full((devices * slot_count,), lower_count, jnp.int32)
    inverse = inverse.at[tile_owner * slot_count + tile_slot].set(
        jnp.arange(lower_count, dtype=jnp.int32)
    )
    my_tiles = lax.dynamic_slice_in_dim(inverse, my_index * slot_count, slot_count, 0)
    present = my_tiles < lower_count
    clipped = jnp.minimum(my_tiles, lower_count - 1)
    lower_i, lower_j = np.tril_indices(tile_count)
    my_rows = jnp.asarray(lower_i, jnp.int32)[clipped]
    my_cols = jnp.asarray(lower_j, jnp.int32)[clipped]
    class_r, my_rowwise = classify(my_rows, my_cols, half_tiles, count_x)
    before = jnp.logical_and(
        class_r[:, None] == class_r[None, :], clipped[None, :] < clipped[:, None]
    )
    before = jnp.logical_and(before, present[None, :])
    my_rank = jnp.minimum(jnp.sum(before.astype(jnp.int32), axis=1), capacity - 1)
    upper_half = incoming[2 * class_r, my_rank]
    lower_half = incoming[2 * class_r + 1, my_rank]
    joined = jnp.concatenate([upper_half, lower_half], axis=1)
    assembled = jnp.where(my_rowwise[:, None, None], joined, jnp.swapaxes(joined, 1, 2))
    return jnp.where(present[:, None, None], assembled, jnp.float32(0.0))


def solution(mesh):
    placed = (P(("gx", "gy"), None), P(), P())
    return jax.shard_map(
        per_device,
        mesh=mesh,
        in_specs=placed,
        out_specs=P(("gx", "gy"), None, None),
        check_vma=False,
    )
```

profile of v0, /device:TPU:1, one launch (start us, length us, event | category | flops | bytes accessed | tf_op | source)
XLA Modules:
  0.0 260.1 jit_solution(4744944973194168256)
XLA Ops:
  6.5 0.7 all-gather.2.cloned.1.call-update
  7.3 5.0 %collective-permute-start.2 = (f32[128,1024]{1,0:T(8,128)}, f32[128,1024]{1,0:T(8,128)S(1)}, u32[]{:S(2)}, u32[]{:S(2)}) collective-permute-start(f32[128,1024]{1,0:T(8,128)} %param.6), channel_id=1, source_target_pairs={{0,48},{16,64},{32,80},{48,96},{64,112},{80,0},{96,16},{112,32},{1... | collective-permute-start | bytes 1572872 | tf_op jit(solution)/shard_map/ppermute | solution.py:11
  12.3 0.7 collective-permute-start.1
  13.3 0.9 collective-permute-start.3
  14.3 0.7 compare_select_fusion
  15.0 11.2 %scatter_custom_fusion = s32[2176]{0:T(1024)S(1)} fusion(s32[2080]{0:T(1024)S(1)} %compare_select_fusion, s32[2080]{0:T(1024)S(1)} %iota.28, s32[]{:T(128)} %constant.151.clone.1), kind=kCustom, calls=%fused_computation.25 | custom fusion | bytes 8708 | tf_op jit(solution)/shard_map/scatter | solution.py:97
  26.3 0.8 fusion.29
  27.1 1.5 gather_fusion.2
  28.9 1.9 bitcast_dynamic-update-slice_fusion.4
  30.9 0.7 fusion.16
  31.7 13.2 %collective-permute-done = f32[128,1024]{1,0:T(8,128)S(1)} collective-permute-done((f32[128,1024]{1,0:T(8,128)}, f32[128,1024]{1,0:T(8,128)S(1)}, u32[]{:S(2)}, u32[]{:S(2)}) %collective-permute-start) | collective-permute-done | bytes 524320 | tf_op jit(solution)/shard_map/ppermute | solution.py:11
  44.9 0.8 bitcast_dynamic-update-slice_fusion.3
  45.7 0.8 bitcast_dynamic-update-slice_fusion.2
  46.6 0.8 bitcast_dynamic-update-slice_fusion.1
  47.4 4.9 %collective-permute-done.3 = f32[128,1024]{1,0:T(8,128)S(1)} collective-permute-done((f32[128,1024]{1,0:T(8,128)}, f32[128,1024]{1,0:T(8,128)S(1)}, u32[]{:S(2)}, u32[]{:S(2)}) %collective-permute-start.3) | collective-permute-done | bytes 524320 | tf_op jit(solution)/shard_map/ppermute | solution.py:11
  52.3 0.8 bitcast_dynamic-update-slice_fusion
  53.1 30.1 %all-gather.2.cloned.1.call-done = f32[2048,1024]{1,0:T(8,128)} async-done(((f32[128,1024]{1,0:T(8,128)}), f32[2048,1024]{1,0:T(8,128)}) %all-gather.2.cloned.1.call-update) | async-done | bytes 8388624 | tf_op jit(solution)/shard_map/all_gather | solution.py:71
  83.2 20.4 %fusion = f32[5,128,2048]{2,1,0:T(8,128)S(1)} fusion(f32[5,128,1024]{2,1,0:T(8,128)} %bitcast_dynamic-update-slice_fusion, f32[2048,1024]{1,0:T(8,128)} %all-gather.2.cloned.1.call-done), kind=kOutput, calls=%fused_computation.8 | convolution fusion | flops 16106127360 | bytes 16252928 | tf_op jit(solution)/shard_map/srk,ck->src/dot_general | solution.py:68
  103.6 3.1 %copy.14 = f32[5,16,8,8,256]{4,3,1,2,0:T(8,128)} copy(f32[5,16,8,8,256]{4,3,2,1,0:T(8,128)S(1)} %bitcast.91) | data formatting | bytes 10485760 | tf_op jit(solution)/shard_map/reshape | solution.py:75
  106.7 5.6 %gather_fusion.3 = f32[33,128,256]{2,1,0:T(8,128)} fusion(f32[5,128,8,256]{3,1,2,0:T(8,128)} %bitcast.90, s32[33]{0:T(128)S(1)} %fusion.16), kind=kCustom, calls=%fused_computation.3 | custom fusion | bytes 8651016 | tf_op jit(solution)/shard_map/gather | solution.py:76
  112.3 5.1 %and_select_fusion = f32[33,128,256]{2,1,0:T(8,128)} fusion(f32[33,128,256]{2,1,0:T(8,128)} %gather_fusion.3, pred[128,256]{1,0:T(8,128)(4,1)S(1)} %iota_compare_fusion, pred[33]{0:T(512)(128)(4,1)S(1)} %get-tuple-element.9), kind=kLoop, calls=%fused_computation.13 | loop fusion | flops 2162688 | bytes 8683553 | tf_op jit(solution)/shard_map/jit(_where)/select_n | solution.py:84
  117.4 3.4 %broadcast_in_dim.74 = f32[16,3,128,256]{3,2,1,0:T(8,128)} broadcast(f32[]{:T(128)} %constant.167.clone.1), dimensions={} | broadcast | bytes 6291460 | tf_op jit(solution)/shard_map/broadcast_in_dim | solution.py:92
  120.8 12.6 %scatter_fusion = f32[16,3,128,256]{3,2,1,0:T(8,128)} fusion(f32[16,3,128,256]{3,2,1,0:T(8,128)} %broadcast_in_dim.74, s32[33]{0:T(128)S(1)} %fusion.25, f32[33,128,256]{2,1,0:T(8,128)} %and_select_fusion), kind=kCustom, calls=%fused_computation.7 | custom fusion | bytes 12976392 | tf_op jit(solution)/shard_map/scatter | solution.py:93
  133.4 5.2 %all-to-all-start = ((f32[16,3,128,256]{3,2,1,0:T(8,128)}), f32[16,3,128,256]{3,2,1,0:T(8,128)}, u32[]{:S(2)}, u32[]{:S(2)}) async-start(f32[16,3,128,256]{3,2,1,0:T(8,128)} %scatter_fusion), calls=%async_computation | async-start | bytes 12582912 | tf_op jit(solution)/shard_map/all_to_all | solution.py:94
  138.6 0.7 gather_fusion.1
  140.3 90.6 %all-to-all-done = f32[16,3,128,256]{3,2,1,0:T(8,128)} async-done(((f32[16,3,128,256]{3,2,1,0:T(8,128)}), f32[16,3,128,256]{3,2,1,0:T(8,128)}, u32[]{:S(2)}, u32[]{:S(2)}) %all-to-all-start) | async-done | bytes 6291488 | tf_op jit(solution)/shard_map/all_to_all | solution.py:94
  230.9 3.5 %gather_fusion.4 = f32[17,128,256]{2,1,0:T(8,128)S(1)} fusion(f32[16,3,128,256]{3,2,1,0:T(8,128)} %all-to-all-done, s32[17]{0:T(128)S(1)} %get-tuple-element.15), kind=kCustom, calls=%fused_computation.4 | custom fusion | bytes 4456584 | tf_op jit(solution)/shard_map/gather | solution.py:112
  234.3 1.6 constant_dynamic-update-slice_fusion.1
  235.9 3.5 %gather_fusion.5 = f32[17,128,256]{2,1,0:T(8,128)S(1)} fusion(f32[16,3,128,256]{3,2,1,0:T(8,128)} %all-to-all-done, s32[17]{0:T(128)S(1)} %get-tuple-element.14), kind=kCustom, calls=%fused_computation.5 | custom fusion | bytes 4456584 | tf_op jit(solution)/shard_map/gather | solution.py:113
  239.4 1.6 constant_dynamic-update-slice_fusion
  241.0 5.7 %copy.11 = f32[17,256,256]{1,2,0:T(8,128)} copy(f32[17,256,256]{2,1,0:T(8,128)} %constant_dynamic-update-slice_fusion) | data formatting | bytes 8912896 | tf_op jit(solution)/shard_map/concatenate | solution.py:114
  246.7 6.6 %fusion.2 = f32[17,256,256]{2,1,0:T(8,128)} fusion(f32[17,256,256]{2,1,0:T(8,128)} %constant_dynamic-update-slice_fusion, f32[17,256,256]{1,2,0:T(8,128)} %copy.11, pred[17]{0:T(512)(128)(4,1)S(1)} %get-tuple-element.6, pred[17]{0:T(512)(128)(4,1)S(1)} %broadcast_compare_fusion), kind=kLoop, calls=%fused_computation.12 | loop fusion | flops 2228224 | bytes 13369378 | tf_op jit(solution)/shard_map/jit(_where)/select_n | solution.py:116
  (32 shorter events, 1.9 us)
Async XLA Ops:
  6.5 76.7 %all-gather.2.cloned.1.call-start = ((), (), s32[]{:S(2)}) async-start(), calls=%async_computation.1 | async-start | bytes 8912896 | tf_op jit(solution)/shard_map/all_gather | solution.py:71
  7.3 39.3 %collective-permute-start.2 = (f32[128,1024]{1,0:T(8,128)}, f32[128,1024]{1,0:T(8,128)S(1)}, u32[]{:S(2)}, u32[]{:S(2)}) collective-permute-start(f32[128,1024]{1,0:T(8,128)} %param.6), channel_id=1, source_target_pairs={{0,48},{16,64},{32,80},{48,96},{64,112},{80,0},{96,16},{112,32},{1... | collective-permute-start | bytes 1572872 | tf_op jit(solution)/shard_map/ppermute | solution.py:11
  12.3 33.4 %collective-permute-start.1 = (f32[128,1024]{1,0:T(8,128)}, f32[128,1024]{1,0:T(8,128)S(1)}, u32[]{:S(2)}, u32[]{:S(2)}) collective-permute-start(f32[128,1024]{1,0:T(8,128)} %param.6), channel_id=1, source_target_pairs={{0,32},{16,48},{32,64},{48,80},{64,96},{80,112},{96,0},{112,16},{1... | collective-permute-start | bytes 1572872 | tf_op jit(solution)/shard_map/ppermute | solution.py:11
  13.0 31.8 %collective-permute-start = (f32[128,1024]{1,0:T(8,128)}, f32[128,1024]{1,0:T(8,128)S(1)}, u32[]{:S(2)}, u32[]{:S(2)}) collective-permute-start(f32[128,1024]{1,0:T(8,128)} %param.6), channel_id=1, source_target_pairs={{0,16},{16,32},{32,48},{48,64},{64,80},{80,96},{96,112},{112,0},{1... | collective-permute-start | bytes 1572872 | tf_op jit(solution)/shard_map/ppermute | solution.py:11
  13.3 39.0 %collective-permute-start.3 = (f32[128,1024]{1,0:T(8,128)}, f32[128,1024]{1,0:T(8,128)S(1)}, u32[]{:S(2)}, u32[]{:S(2)}) collective-permute-start(f32[128,1024]{1,0:T(8,128)} %param.6), channel_id=1, source_target_pairs={{0,64},{16,80},{32,96},{48,112},{64,0},{80,16},{96,32},{112,48},{1... | collective-permute-start | bytes 1572872 | tf_op jit(solution)/shard_map/ppermute | solution.py:11
  133.4 5.2 %copy-start.1 = (s32[2080]{0:T(1024)S(1)}, s32[2080]{0:T(1024)}, u32[]{:S(2)}) copy-start(s32[2080]{0:T(1024)} %constant.174.clone) | copy-start | bytes 24964
  133.4 5.9 %copy-start = (s32[2080]{0:T(1024)S(1)}, s32[2080]{0:T(1024)}, u32[]{:S(2)}) copy-start(s32[2080]{0:T(1024)} %constant.173.clone) | copy-start | bytes 24964
  133.4 97.5 %all-to-all-start = ((f32[16,3,128,256]{3,2,1,0:T(8,128)}), f32[16,3,128,256]{3,2,1,0:T(8,128)}, u32[]{:S(2)}, u32[]{:S(2)}) async-start(f32[16,3,128,256]{3,2,1,0:T(8,128)} %scatter_fusion), calls=%async_computation | async-start | bytes 12582912 | tf_op jit(solution)/shard_map/all_to_all | solution.py:94
Sparse Core Ops, SparseCore 0:
  9.5 73.6 all-gather.1
where the time goes:
time: 261 us; the launch traced here: 260 us
  waiting for transfers between devices  139 us (53%)
  local copies, waits for them, and re-layouts  59.9 us (23%)
  matrix products  20.4 us (8%)
  other arithmetic  14.7 us (6%)
  between operations  13.5 us (5%)
  starting transfers between devices  12.1 us (5%)
    all_to_all x1, waiting for transfers between devices, per_device(): lax.all_to_all(outgoing, 'gy', split_axis=0, concat_axis=0, tiled=True)  90.6 us
    all_gather x1, waiting for transfers between devices, per_device(): lax.all_gather(matrix_rows, 'gy', axis=0, tiled=True)  30.1 us
    dot_general x1, matrix products, per_device(): jnp.einsum('srk,ck->src', stacked, lax.all_gather(matrix_rows, 'gy', axis...  20.4 us
    ppermute x4, waiting for transfers between devices, from_behind(): return lax.ppermute(value, axis, pairs)  18.1 us
    scatter x1, local copies, waits for them, and re-layouts, per_device(): outgoing = outgoing.at[target, rank].set(pieces, mode='drop')  12.6 us
    scatter x1, local copies, waits for them, and re-layouts, per_device(): inverse.at[tile_owner * slot_count + tile_slot]  11.2 us
    concatenate x2, local copies, waits for them, and re-layouts, per_device(): joined = jnp.concatenate([upper_half, lower_half], axis=1)  7.29 us
    ppermute x4, starting transfers between devices, from_behind(): return lax.ppermute(value, axis, pairs)  6.94 us
  transfers between devices with their start and end apart: 6, of which 4 were waited for; matrix products, arithmetic and copies ran while one was open for 9% of the time, Pallas kernels for 0%

commit v1 on v0

v1 whole, which is shorter than its diff:
```python
import functools

import jax
import jax.numpy as jnp
import numpy as np
from jax import lax
from jax.experimental import pallas as pl
from jax.experimental.pallas import tpu as pltpu
from jax.sharding import PartitionSpec as P

MESH = pl.DeviceIdType.MESH
SIDE = 4
PLANE = SIDE * SIDE
GROUPS = 8
HALF_TILES = 8
STEPS = 5
CAP = 3
CHUNK = 128
TILE = 256
TILE_COUNT = 64


def exchange_kernel(
    step_tab, col_tab, diag_tab, a_ref, in_ref,
    g, ghi, glo, rf, rhi, rlo, outs,
    a1_send, a1_recv, a2_send, a2_recv, b1_send, b1_recv, b2_send, b2_recv,
    z_send, z_recv, p_send, p_recv, x_send, x_recv, l_sem,
):
    gx = lax.axis_index("gx")
    gy = lax.axis_index("gy")
    core = gx % 2
    y = gy // SIDE
    x = gy % SIDE
    u = jnp.where(core == 0, x, y)
    v = jnp.where(core == 0, y, x)
    stride_u = jnp.where(core == 0, 1, SIDE)
    stride_v = jnp.where(core == 0, SIDE, 1)

    def at(du, dv):
        return (u + du + SIDE) % SIDE * stride_u + (v + dv + SIDE) % SIDE * stride_v

    ahead = (gx + 2) % GROUPS
    behind = (gx + 6) % GROUPS
    partner = gx + 1 - 2 * core

    barrier = pltpu.get_barrier_semaphore()

    def greet(i, carry):
        pl.semaphore_signal(
            barrier, inc=1, device_id={"gx": gx, "gy": (gy + i) % PLANE}, device_id_type=MESH
        )
        return carry

    lax.fori_loop(1, PLANE, greet, 0)
    for other in (ahead, behind, partner):
        pl.semaphore_signal(barrier, inc=1, device_id={"gx": other, "gy": gy}, device_id_type=MESH)
    pl.semaphore_wait(barrier, PLANE + 2)

    def whole(c):
        return g.at[c // 2, pl.ds(pl.multiple_of(c % 2 * CHUNK, CHUNK), CHUNK)]

    def half(c, h):
        start = pl.multiple_of(c % 2 * CHUNK + h * (CHUNK // 2), CHUNK // 2)
        return g.at[c // 2, pl.ds(start, CHUNK // 2)]

    def remote(src, dst, send, recv, to_gx, to_gy):
        return pltpu.make_async_remote_copy(
            src_ref=src, dst_ref=dst, send_sem=send, recv_sem=recv,
            device_id={"gx": to_gx, "gy": to_gy}, device_id_type=MESH,
        )

    me = gy
    a1 = [remote(a_ref, whole(me), a1_send.at[d], a1_recv.at[d], gx, at(1 - 2 * d, 0)) for d in (0, 1)]
    z1 = remote(a_ref, rf.at[1], z_send.at[0], z_recv.at[0], ahead, gy)
    offs = (0, -1, 1, 2)
    b1 = []
    for n, du in enumerate(offs):
        src = a_ref if n == 0 else whole(at(du, 0))
        b1.append([
            remote(src, whole(at(du, 0)), b1_send.at[n, d], b1_recv.at[n, d], gx, at(0, 1 - 2 * d))
            for d in (0, 1)
        ])
    a1[0].start()
    a1[1].start()
    b1[0][0].start()
    b1[0][1].start()
    z1.start()

    def split_g(c):
        block = c // 2
        rows = pl.ds(pl.multiple_of(c % 2 * CHUNK, CHUNK), CHUNK)
        value = g[block, rows, :]
        high = value.astype(jnp.bfloat16)
        ghi[block, rows, :] = high
        glo[block, rows, :] = (value - high.astype(jnp.float32)).astype(jnp.bfloat16)

    def split_r(n, value):
        high = value.astype(jnp.bfloat16)
        rhi[n] = high
        rlo[n] = (value - high.astype(jnp.float32)).astype(jnp.bfloat16)

    own = a_ref[...]
    split_r(0, own)
    block, rows = me // 2, pl.ds(pl.multiple_of(me % 2 * CHUNK, CHUNK), CHUNK)
    ghi[block, rows, :] = rhi[0]
    glo[block, rows, :] = rlo[0]

    a2 = []
    for d in (0, 1):
        src_c = at(-1 + 2 * d, 0)
        a1[d].wait_recv()
        copy = remote(half(src_c, d), half(src_c, d), a2_send.at[d], a2_recv.at[d], gx, at(1 - 2 * d, 0))
        copy.start()
        a2.append(copy)
        b1[1 + d][0].start()
        b1[1 + d][1].start()
        split_g(src_c)

    z1.wait_recv()
    z2 = remote(rf.at[1], rf.at[3], z_send.at[1], z_recv.at[1], ahead, gy)
    z2.start()

    b2 = []

    def forward_v(n):
        for d in (0, 1):
            c = at(offs[n], -1 + 2 * d)
            b1[n][d].wait_recv()
            copy = remote(half(c, d), half(c, d), b2_send.at[n, d], b2_recv.at[n, d], gx, at(0, 1 - 2 * d))
            copy.start()
            b2.append(copy)
            split_g(c)

    forward_v(0)
    for d in (0, 1):
        a2[d].wait_recv()
    b1[3][0].start()
    b1[3][1].start()
    split_g(at(2, 0))

    @pl.when(core == 0)
    def _():
        remote(a_ref, rf.at[0], p_send.at[0], p_recv.at[0], partner, gy).start()

    @pl.when(core == 1)
    def _():
        remote(rf.at[1], rf.at[0], p_send.at[0], p_recv.at[0], partner, gy).start()

    split_r(2, rf[1])
    forward_v(1)
    z2.wait_recv()

    @pl.when(core == 0)
    def _():
        remote(rf.at[1], rf.at[2], p_send.at[1], p_recv.at[1], partner, gy).start()

    @pl.when(core == 1)
    def _():
        remote(rf.at[3], rf.at[2], p_send.at[1], p_recv.at[1], partner, gy).start()

    split_r(4, rf[3])
    forward_v(2)
    p1 = remote(a_ref, rf.at[0], p_send.at[0], p_recv.at[0], partner, gy)
    p2 = remote(a_ref, rf.at[2], p_send.at[1], p_recv.at[1], partner, gy)
    p1.wait_recv()
    split_r(1, rf[0])
    p2.wait_recv()
    split_r(3, rf[2])
    forward_v(3)
    for n in range(4):
        for d in (0, 1):
            b2[2 * n + d].wait_recv()
        split_g(at(offs[n], 2))

    row_in = lax.broadcasted_iota(jnp.int32, (CHUNK, TILE), 0) + gy % 2 * CHUNK
    col_in = lax.broadcasted_iota(jnp.int32, (CHUNK, TILE), 1)
    upper = row_in < col_in

    def dot(p, q):
        return lax.dot_general(p, q, (((1,), (1,)), ((), ())), preferred_element_type=jnp.float32)

    def one_owner(i, carry):
        order = (PLANE // 2 + 1 + i) % PLANE
        to = (gy + order) % PLANE

        def one_slot(k, inner):
            entry = to * CAP + k
            s = step_tab[entry]
            j = col_tab[entry]
            rh = rhi[s]
            gh = ghi[j]
            value = dot(rh, gh) + dot(rh, glo[j]) + dot(rlo[s], gh)
            masked = jnp.logical_and(upper, diag_tab[entry] > 0)
            outs[order, k] = jnp.where(masked, jnp.float32(0.0), value)
            return inner

        lax.fori_loop(0, CAP, one_slot, 0)

        @pl.when(order > 0)
        def _():
            remote(outs.at[order], in_ref.at[gy], x_send.at[order], x_recv.at[order], gx, to).start()

        return carry

    lax.fori_loop(0, PLANE, one_owner, 0)
    local = pltpu.make_async_copy(outs.at[0], in_ref.at[gy], l_sem)
    local.start()

    for copy in a1 + a2 + b2 + [z1, z2, p1, p2] + [c for pair in b1 for c in pair]:
        copy.wait_send()
    local.wait()

    def finish(i, carry):
        source = (gy + PLANE - i) % PLANE
        copy = remote(outs.at[i], in_ref.at[source], x_send.at[i], x_recv.at[i], gx, (gy + i) % PLANE)
        copy.wait_send()
        copy.wait_recv()
        return carry

    lax.fori_loop(1, PLANE, finish, 0)


def exchange(matrix_rows, step_tab, col_tab, diag_tab):
    width = matrix_rows.shape[1]
    smem = pl.BlockSpec(memory_space=pltpu.SMEM)
    dma = pltpu.SemaphoreType.DMA
    return pl.pallas_call(
        exchange_kernel,
        out_shape=jax.ShapeDtypeStruct((PLANE, CAP, CHUNK, TILE), jnp.float32),
        in_specs=[smem, smem, smem, pl.BlockSpec(memory_space=pltpu.VMEM)],
        out_specs=pl.BlockSpec(memory_space=pl.ANY),
        scratch_shapes=[
            pltpu.VMEM((HALF_TILES, TILE, width), jnp.float32),
            pltpu.VMEM((HALF_TILES, TILE, width), jnp.bfloat16),
            pltpu.VMEM((HALF_TILES, TILE, width), jnp.bfloat16),
            pltpu.VMEM((4, CHUNK, width), jnp.float32),
            pltpu.VMEM((STEPS, CHUNK, width), jnp.bfloat16),
            pltpu.VMEM((STEPS, CHUNK, width), jnp.bfloat16),
            pltpu.VMEM((PLANE, CAP, CHUNK, TILE), jnp.float32),
            dma((2,)), dma((2,)), dma((2,)), dma((2,)),
            dma((4, 2)), dma((4, 2)), dma((4, 2)), dma((4, 2)),
            dma((2,)), dma((2,)), dma((2,)), dma((2,)),
            dma((PLANE,)), dma((PLANE,)), dma(()),
        ],
        compiler_params=pltpu.CompilerParams(
            collective_id=0, has_side_effects=True, vmem_limit_bytes=48 * 1024 * 1024
        ),
        name="exchange",
    )(step_tab, col_tab, diag_tab, matrix_rows)


def assemble_kernel(src_tab, rank_tab, kind_tab, upper_ref, lower_ref, out_ref):
    kind = kind_tab[pl.program_id(0)]

    @pl.when(kind == 0)
    def _():
        out_ref[...] = jnp.zeros_like(out_ref)

    @pl.when(kind == 1)
    def _():
        out_ref[0, :CHUNK, :] = upper_ref[0, 0]
        out_ref[0, CHUNK:, :] = lower_ref[0, 0]

    @pl.when(kind == 2)
    def _():
        out_ref[0, :, :CHUNK] = upper_ref[0, 0].T
        out_ref[0, :, CHUNK:] = lower_ref[0, 0].T


def assemble(incoming, class_r, rank, kind):
    slots = class_r.shape[0]

    def piece(h):
        return pl.BlockSpec(
            (1, 1, CHUNK, TILE), lambda q, src, rk, kd: (2 * src[q] + h, rk[q], 0, 0)
        )

    return pl.pallas_call(
        assemble_kernel,
        out_shape=jax.ShapeDtypeStruct((slots, TILE, TILE), jnp.float32),
        grid_spec=pltpu.PrefetchScalarGridSpec(
            num_scalar_prefetch=3,
            grid=(slots,),
            in_specs=[piece(0), piece(1)],
            out_specs=pl.BlockSpec((1, TILE, TILE), lambda q, src, rk, kd: (q, 0, 0)),
        ),
        name="assemble",
    )(class_r, rank, kind, incoming, incoming)


def send_tables(x_index, y_index, tile_owner):
    own_r = y_index // 2
    quarter = HALF_TILES // 2
    middle = GROUPS // 2 - 1
    offsets = jnp.arange(quarter + 1, dtype=jnp.int32)
    first_cols = (own_r - offsets) % HALF_TILES
    first_valid = jnp.logical_or(offsets < quarter, own_r < quarter)
    flag = (x_index >= GROUPS // 2).astype(jnp.int32)
    last_cols = 2 * jnp.arange(quarter, dtype=jnp.int32) + (own_r + flag) % 2
    middle_cols = jnp.asarray(np.tile(np.arange(HALF_TILES, dtype=np.int32), middle))
    col_of = jnp.concatenate([first_cols, middle_cols, last_cols])
    valid = jnp.concatenate([first_valid, jnp.ones((middle * HALF_TILES + quarter,), bool)])
    step_of = jnp.asarray(np.concatenate([
        np.zeros(quarter + 1, np.int32),
        np.repeat(np.arange(1, middle + 1, dtype=np.int32), HALF_TILES),
        np.full(quarter, middle + 1, np.int32),
    ]))
    source_x = (x_index - step_of) % GROUPS
    rowwise = jnp.where(step_of == 0, col_of <= own_r, source_x > x_index)
    near = source_x * HALF_TILES + own_r
    far = x_index * HALF_TILES + col_of
    row_tile = jnp.where(rowwise, near, far)
    col_tile = jnp.where(rowwise, far, near)
    tile_index = jnp.where(valid, row_tile * (row_tile + 1) // 2 + col_tile, 0)
    target = jnp.where(valid, tile_owner[tile_index] % PLANE, PLANE)
    earlier = (target[:, None] == target[None, :]) & (tile_index[None, :] < tile_index[:, None])
    earlier = earlier & valid[None, :]
    rank = jnp.sum(earlier.astype(jnp.int32), axis=1)
    place = jnp.where(valid, target * CAP + rank, PLANE * CAP)
    hit = place[None, :] == jnp.arange(PLANE * CAP, dtype=jnp.int32)[:, None]
    packed = step_of * 16 + col_of * 2 + (row_tile == col_tile).astype(jnp.int32)
    chosen = jnp.sum(jnp.where(hit, packed[None, :], 0), axis=1)
    return chosen // 16, chosen // 2 % HALF_TILES, chosen % 2


def receive_tables(my_index, slot_count, tile_owner, tile_slot):
    lower_i, lower_j = np.tril_indices(TILE_COUNT)
    code = jnp.asarray(lower_i * TILE_COUNT + lower_j, jnp.int32)
    wanted = jnp.arange(slot_count, dtype=jnp.int32)
    hit = (tile_owner == my_index)[None, :] & (tile_slot[None, :] == wanted[:, None])
    found = jnp.max(jnp.where(hit, code[None, :], -1), axis=1)
    present = found >= 0
    clipped = jnp.maximum(found, 0)
    row_tile = clipped // TILE_COUNT
    col_tile = clipped % TILE_COUNT
    group_a = row_tile // HALF_TILES
    group_b = col_tile // HALF_TILES
    inner_i = row_tile % HALF_TILES
    inner_j = col_tile % HALF_TILES
    gap = group_a - group_b
    across = (gap > GROUPS // 2) | ((gap == GROUPS // 2) & ((inner_i + inner_j) % 2 == 0))
    rowwise = jnp.where(gap == 0, inner_i - inner_j < HALF_TILES // 2, across)
    class_r = jnp.where(rowwise, inner_i, inner_j)
    before = (class_r[:, None] == class_r[None, :]) & (clipped[None, :] < clipped[:, None])
    before = before & present[None, :]
    rank = jnp.minimum(jnp.sum(before.astype(jnp.int32), axis=1), CAP - 1)
    kind = jnp.where(present, jnp.where(rowwise, 1, 2), 0)
    return class_r, rank, kind


def per_device(matrix_rows, tile_owner, tile_slot):
    x_index = lax.axis_index("gx")
    y_index = lax.axis_index("gy")
    devices = GROUPS * PLANE
    slot_count = (tile_owner.shape[0] + devices - 1) // devices
    step_tab, col_tab, diag_tab = send_tables(x_index, y_index, tile_owner)
    class_r, rank, kind = receive_tables(x_index * PLANE + y_index, slot_count, tile_owner, tile_slot)
    incoming = exchange(matrix_rows, step_tab, col_tab, diag_tab)
    return assemble(incoming, class_r, rank, kind)


def solution(mesh):
    placed = (P(("gx", "gy"), None), P(), P())
    return jax.shard_map(
        per_device,
        mesh=mesh,
        in_specs=placed,
        out_specs=P(("gx", "gy"), None, None),
        check_vma=False,
    )
```

time: 261 us -> 180 us (0.69)
  Pallas kernels: 0 us -> 171 us
  waiting for transfers between devices: 139 us -> 0 us
  local copies, waits for them, and re-layouts: 59.9 us -> 2.53 us
  matrix products: 20.4 us -> 0 us
  between operations: 13.5 us -> 0.06 us
  starting transfers between devices: 12.1 us -> 0 us
  other arithmetic: 14.7 us -> 4.82 us
    pallas_call x0 -> x2, Pallas kernels: none -> 171 us  [the longest x1 159 us: exchange(): pl.pallas_call(exchange_kernel, out_shape=jax.ShapeDtypeStruct((PLANE, CA...]
    all_to_all x1 -> x0, waiting for transfers between devices: 90.6 us -> none  [per_device(): lax.all_to_all(outgoing, 'gy', split_axis=0, concat_axis=0, tiled=True)]
    all_gather x1 -> x0, waiting for transfers between devices: 30.1 us -> none  [per_device(): lax.all_gather(matrix_rows, 'gy', axis=0, tiled=True)]
    scatter x2 -> x0, local copies, waits for them, and re-layouts: 23.7 us -> none  [the longest x1 12.6 us: per_device(): outgoing = outgoing.at[target, rank].set(pieces, mode='drop')]
    dot_general x1 -> x0, matrix products: 20.4 us -> none  [per_device(): jnp.einsum('srk,ck->src', stacked, lax.all_gather(matrix_rows, 'gy', axis...]
    ppermute x4 -> x0, waiting for transfers between devices: 18.1 us -> none  [from_behind(): return lax.ppermute(value, axis, pairs)]
    gather x6 -> x1, local copies, waits for them, and re-layouts: 15.5 us -> 1.48 us  [send_tables(): target = jnp.where(valid, tile_owner[tile_index] % PLANE, PLANE)]
    select_n x8 -> x6, other arithmetic: 12.6 us -> 1.39 us  [the longest x2 0.8 us: send_tables(): target = jnp.where(valid, tile_owner[tile_index] % PLANE, PLANE)]
  transfers between devices with their start and end apart: 6 -> 0, of which waited for: 4 -> 0; matrix products, arithmetic and copies ran while one was open for 9% -> 0% of each run, Pallas kernels for 0% -> 0%
where the time goes in v1:
time: 180 us; the launch traced here: 178 us
  Pallas kernels  171 us (95%)
  other arithmetic  4.82 us (3%)
  local copies, waits for them, and re-layouts  2.53 us (1%)
    pallas_call x1, Pallas kernels, exchange(): pl.pallas_call(exchange_kernel, out_shape=jax.ShapeDtypeStruct((PLANE, CA...  159 us
    pallas_call x1, Pallas kernels, assemble(): pl.pallas_call(assemble_kernel, out_shape=jax.ShapeDtypeStruct((slots, TI...  11.8 us

profile of v1, /device:TPU:1, one launch (start us, length us, event | category | flops | bytes accessed | tf_op | source)
XLA Modules:
  0.0 178.0 jit_solution(4817456978527456110)
XLA Ops:
  0.0 0.8 compare_select_fusion
  0.8 0.7 broadcast_compare_fusion
  1.5 0.9 select_reduce_fusion
  2.4 0.5 select_select_fusion
  3.0 0.0 copy-start.1
  3.0 0.2 convert_reduce_fusion.1
  3.2 0.6 broadcast_minimum_fusion.rank_tab
  3.8 1.5 gather_fusion
  5.3 0.2 convert_reduce_fusion
  5.5 0.8 fusion.3
  6.2 0.1 select_reduce_fusion.1
  6.3 0.0 copy-start
  6.4 1.0 copy-done
  7.4 158.8 %exchange.1.upper_ref.lower_ref = f32[16,3,128,256]{3,2,1,0:T(8,128)} custom-call(s32[48]{0:T(128)S(1)} %get-tuple-element.13.step_tab, s32[48]{0:T(128)S(1)} %get-tuple-element.12.col_tab, s32[48]{0:T(128)S(1)} %get-tuple-element.11.diag_tab, f32[128,1024]{1,0:T(8,128)S(1)} %copy-done), custom_call_target="tpu_custom_call" | custom-call | tf_op jit(solution)/shard_map/exchange/pallas_call | solution.py:227
  166.2 0.0 copy-done.1
  166.2 11.8 %assemble.1 = f32[17,256,256]{2,1,0:T(8,128)} custom-call(s32[17]{0:T(128)} %copy-done.1, s32[17]{0:T(128)} %broadcast_minimum_fusion.rank_tab, s32[17]{0:T(128)} %get-tuple-element.9.kind_tab, f32[16,3,128,256]{3,2,1,0:T(8,128)} %exchange.1.upper_ref.lower_ref, f32[16,3,128,256]{3,2,1,0:T(8,128)} %exchange.1.upper_ref.lower_ref), custom_call_target="tpu_custom_call" | custom-call | tf_op jit(solution)/shard_map/assemble/pallas_call | solution.py:278
  (9 shorter events, 0.1 us)
Async XLA Ops:
  3.0 163.2 %copy-start.1 = (s32[17]{0:T(128)}, s32[17]{0:T(128)S(1)}, u32[]{:S(2)}) copy-start(s32[17]{0:T(128)S(1)} %fusion.8.src_tab) | copy-start | bytes 208
  6.3 1.0 copy-start

commit v2 on v1

v2 whole, which is shorter than its diff:
```python
import jax
import jax.numpy as jnp
import numpy as np
from jax import lax
from jax.experimental import pallas as pl
from jax.experimental.pallas import tpu as pltpu
from jax.sharding import PartitionSpec as P

MESH = pl.DeviceIdType.MESH
SIDE = 4
PLANE = SIDE * SIDE
GROUPS = 8
HALF_TILES = 8
STEPS = 5
CAP = 3
CHUNK = 128
HALF = CHUNK // 2
TILE = 256
TILE_COUNT = 64
ENTRIES = 33
ORDER = (
    (2, 2), (1, 0), (3, 0), (0, 2), (1, 1), (3, 3), (2, 0), (0, 1),
    (0, 3), (1, 2), (3, 2), (1, 3), (3, 1), (2, 1), (2, 3), (0, 0),
)


def entry_of(e, gx, r):
    quarter = HALF_TILES // 2
    middle = GROUPS // 2 - 1
    if e <= quarter:
        s, col = 0, (r - e + HALF_TILES) % HALF_TILES
        valid = r < quarter if e == quarter else None
        rowwise = col <= r
        source = gx
    elif e <= quarter + middle * HALF_TILES:
        s, col = 1 + (e - quarter - 1) // HALF_TILES, (e - quarter - 1) % HALF_TILES
        valid = None
        source = (gx - s + GROUPS) % GROUPS
        rowwise = source > gx
    else:
        s = middle + 1
        last = e - quarter - 1 - middle * HALF_TILES
        col = 2 * last + (r + jnp.where(gx >= GROUPS // 2, 1, 0)) % 2
        valid = None
        source = (gx - s + GROUPS) % GROUPS
        rowwise = source > gx
    near = source * HALF_TILES + r
    far = gx * HALF_TILES + col
    row_tile = jnp.where(rowwise, near, far)
    col_tile = jnp.where(rowwise, far, near)
    return s, col, valid, rowwise, row_tile, col_tile


def exchange_kernel(
    owner_smem, owner_ref, slot_ref, code_ref, a_ref, in_ref, table_ref,
    g, ghi, glo, rf, rhi, rlo, outs, target_tab, entry_tab, send_tab, found_tab,
    a1_send, a1_recv, a2_send, a2_recv, b1_send, b1_recv, b2_send, b2_recv,
    z_send, z_recv, p_send, p_recv, x_send, x_recv, l_sem,
):
    gx = lax.axis_index("gx")
    gy = lax.axis_index("gy")
    core = gx % 2
    y = gy // SIDE
    x = gy % SIDE
    u = jnp.where(core == 0, x, y)
    v = jnp.where(core == 0, y, x)
    stride_u = jnp.where(core == 0, 1, SIDE)
    stride_v = jnp.where(core == 0, SIDE, 1)

    def at(du, dv):
        return (u + du + SIDE) % SIDE * stride_u + (v + dv + SIDE) % SIDE * stride_v

    ahead = (gx + 2) % GROUPS
    behind = (gx + 6) % GROUPS
    partner = gx + 1 - 2 * core

    barrier = pltpu.get_barrier_semaphore()

    def greet(i, carry):
        pl.semaphore_signal(
            barrier, inc=1, device_id={"gx": gx, "gy": (gy + i) % PLANE}, device_id_type=MESH
        )
        return carry

    lax.fori_loop(1, PLANE, greet, 0)
    for other in (ahead, behind, partner):
        pl.semaphore_signal(barrier, inc=1, device_id={"gx": other, "gy": gy}, device_id_type=MESH)
    pl.semaphore_wait(barrier, PLANE + 2)

    def half(c, h):
        start = pl.multiple_of(c % 2 * CHUNK + h * HALF, HALF)
        return g.at[c // 2, pl.ds(start, HALF)]

    def own_half(h):
        return a_ref.at[pl.ds(h * HALF, HALF)]

    def remote(src, dst, send, recv, to_gx, to_gy):
        return pltpu.make_async_remote_copy(
            src_ref=src, dst_ref=dst, send_sem=send, recv_sem=recv,
            device_id={"gx": to_gx, "gy": to_gy}, device_id_type=MESH,
        )

    copies = []

    def start(copy):
        copy.start()
        copies.append(copy)

    me = gy
    a1 = [[
        remote(own_half(h), half(me, h), a1_send.at[d, p], a1_recv.at[d, p], gx, at(1 - 2 * d, 0))
        for p, h in enumerate((d, 1 - d))
    ] for d in (0, 1)]
    a2 = [
        remote(
            half(at(-1 + 2 * d, 0), d), half(at(-1 + 2 * d, 0), d),
            a2_send.at[d], a2_recv.at[d], gx, at(1 - 2 * d, 0),
        )
        for d in (0, 1)
    ]
    offs = (0, -1, 1, 2)
    b1 = [[[
        remote(
            own_half(h) if n == 0 else half(at(du, 0), h), half(at(du, 0), h),
            b1_send.at[n, d, p], b1_recv.at[n, d, p], gx, at(0, 1 - 2 * d),
        )
        for p, h in enumerate((d, 1 - d))
    ] for d in (0, 1)] for n, du in enumerate(offs)]
    b2 = [[
        remote(
            half(at(du, -1 + 2 * d), d), half(at(du, -1 + 2 * d), d),
            b2_send.at[n, d], b2_recv.at[n, d], gx, at(0, 1 - 2 * d),
        )
        for d in (0, 1)
    ] for n, du in enumerate(offs)]
    z1 = remote(a_ref, rf.at[1], z_send.at[0], z_recv.at[0], ahead, gy)
    z2 = remote(rf.at[1], rf.at[3], z_send.at[1], z_recv.at[1], ahead, gy)
    for p in (0, 1):
        for d in (0, 1):
            start(a1[d][p])
    start(z1)
    for p in (0, 1):
        for d in (0, 1):
            start(b1[0][d][p])

    def split_g(c):
        block = c // 2
        rows = pl.ds(pl.multiple_of(c % 2 * CHUNK, CHUNK), CHUNK)
        value = g[block, rows, :]
        high = value.astype(jnp.bfloat16)
        ghi[block, rows, :] = high
        glo[block, rows, :] = (value - high.astype(jnp.float32)).astype(jnp.bfloat16)

    def split_r(n, value):
        high = value.astype(jnp.bfloat16)
        rhi[n] = high
        rlo[n] = (value - high.astype(jnp.float32)).astype(jnp.bfloat16)

    own_r = gy // 2
    for e in range(ENTRIES):
        s, col, valid, rowwise, row_tile, col_tile = entry_of(e, gx, own_r)
        owner = owner_smem[row_tile * (row_tile + 1) // 2 + col_tile] % PLANE
        target_tab[e] = owner if valid is None else jnp.where(valid, owner, -1)
        diag = jnp.where(row_tile == col_tile, 2, 0)
        entry_tab[e] = s * 32 + col * 4 + diag + jnp.where(rowwise, 1, 0)

    def fill(to, carry):
        kept = [jnp.int32(0)] * CAP
        for e in range(ENTRIES):
            hit = target_tab[e] == to
            fresh = entry_tab[e]
            kept = [jnp.where(hit, b, a) for a, b in zip(kept, [fresh] + kept[:-1])]
        for k in range(CAP):
            send_tab[to * CAP + k] = kept[k]
        return carry

    lax.fori_loop(0, PLANE, fill, 0)

    split_r(0, a_ref[...])
    block, rows = me // 2, pl.ds(pl.multiple_of(me % 2 * CHUNK, CHUNK), CHUNK)
    ghi[block, rows, :] = rhi[0]
    glo[block, rows, :] = rlo[0]

    for d in (0, 1):
        a1[d][0].wait_recv()
        start(a2[d])
    for d in (0, 1):
        a1[d][1].wait_recv()
        for p in (0, 1):
            for e in (0, 1):
                start(b1[1 + d][e][p])
        split_g(at(-1 + 2 * d, 0))

    z1.wait_recv()
    start(z2)

    def forward_v(n):
        for d in (0, 1):
            b1[n][d][0].wait_recv()
            start(b2[n][d])

    def take_v(n):
        for d in (0, 1):
            b1[n][d][1].wait_recv()
            split_g(at(offs[n], -1 + 2 * d))

    mine = owner_ref[...] == gx * PLANE + gy
    slots = table_ref.shape[0]

    def find(q, carry):
        hit = jnp.logical_and(mine, slot_ref[...] == q)
        found = jnp.max(jnp.where(hit, code_ref[...], -1))
        row_tile = jnp.maximum(found, 0) // TILE_COUNT
        col_tile = jnp.maximum(found, 0) % TILE_COUNT
        group_a, inner_i = row_tile // HALF_TILES, row_tile % HALF_TILES
        group_b, inner_j = col_tile // HALF_TILES, col_tile % HALF_TILES
        gap = group_a - group_b
        even = (inner_i + inner_j) % 2 == 0
        across = jnp.logical_or(gap > GROUPS // 2, jnp.logical_and(gap == GROUPS // 2, even))
        within = inner_i - inner_j < HALF_TILES // 2
        rowwise = jnp.logical_or(jnp.logical_and(gap == 0, within), jnp.logical_and(gap > 0, across))
        class_r = jnp.where(rowwise, inner_i, inner_j)
        col = jnp.where(rowwise, inner_j, inner_i)
        s = (gx - jnp.where(rowwise, group_a, group_b) + GROUPS) % GROUPS
        place = s * HALF_TILES + jnp.where(s == 0, (class_r - col + HALF_TILES) % HALF_TILES, col)
        found_tab[q] = jnp.where(found >= 0, class_r * 64 + place, -1)
        table_ref[q] = jnp.where(found >= 0, jnp.where(rowwise, 1, 2), 0) + class_r * 4
        return carry

    lax.fori_loop(0, slots, find, 0)

    def count(q, carry):
        own = found_tab[q]
        later = jnp.int32(0)
        for other in range(slots):
            code = found_tab[other]
            same = jnp.logical_and(code // 64 == own // 64, code > own)
            later = later + jnp.where(same, 1, 0)
        table_ref[q] = table_ref[q] + 32 * jnp.minimum(later, CAP - 1)
        return carry

    forward_v(0)
    for d in (0, 1):
        a2[d].wait_recv()
        start(b1[3][d][0])
    for d in (0, 1):
        start(b1[3][d][1])
    split_g(at(2, 0))

    @pl.when(core == 0)
    def _():
        remote(a_ref, rf.at[0], p_send.at[0], p_recv.at[0], partner, gy).start()

    @pl.when(core == 1)
    def _():
        remote(rf.at[1], rf.at[0], p_send.at[0], p_recv.at[0], partner, gy).start()

    take_v(0)
    lax.fori_loop(0, slots, count, 0)
    split_r(2, rf[1])
    forward_v(1)
    z2.wait_recv()

    @pl.when(core == 0)
    def _():
        remote(rf.at[1], rf.at[2], p_send.at[1], p_recv.at[1], partner, gy).start()

    @pl.when(core == 1)
    def _():
        remote(rf.at[3], rf.at[2], p_send.at[1], p_recv.at[1], partner, gy).start()

    take_v(1)
    split_r(4, rf[3])
    forward_v(2)
    p1 = remote(a_ref, rf.at[0], p_send.at[0], p_recv.at[0], partner, gy)
    p2 = remote(a_ref, rf.at[2], p_send.at[1], p_recv.at[1], partner, gy)
    p1.wait_recv()
    split_r(1, rf[0])
    take_v(2)
    forward_v(3)
    p2.wait_recv()
    split_r(3, rf[2])
    take_v(3)
    for n in range(4):
        for d in (0, 1):
            b2[n][d].wait_recv()
        split_g(at(offs[n], 2))

    row_in = lax.broadcasted_iota(jnp.int32, (CHUNK, TILE), 0) + gy % 2 * CHUNK
    col_in = lax.broadcasted_iota(jnp.int32, (CHUNK, TILE), 1)
    upper = row_in < col_in

    def dot(p, q):
        return lax.dot_general(p, q, (((1,), (1,)), ((), ())), preferred_element_type=jnp.float32)

    def one_piece(i, carry):
        k = i // PLANE
        n = i % PLANE
        first = jnp.int32(0)
        second = jnp.int32(0)
        for m, (one, two) in enumerate(ORDER):
            first = jnp.where(n == m, one, first)
            second = jnp.where(n == m, two, second)
        dy = jnp.where(core == 0, first, second)
        dx = jnp.where(core == 0, second, first)
        to = (y + dy) % SIDE * SIDE + (x + dx) % SIDE
        order = dy * SIDE + dx
        entry = send_tab[to * CAP + k]
        s = entry // 32
        j = entry // 4 % HALF_TILES
        rh = rhi[s]
        gh = ghi[j]
        value = dot(rh, gh) + dot(rh, glo[j]) + dot(rlo[s], gh)
        masked = jnp.logical_and(upper, entry // 2 % 2 > 0)
        value = jnp.where(masked, jnp.float32(0.0), value)
        rowwise = jnp.full((CHUNK, CHUNK), entry % 2, jnp.int32) > 0
        for c in range(2):
            part = value[:, c * CHUNK:(c + 1) * CHUNK]
            outs[order, k, c] = jnp.where(rowwise, part, part.T)

        @pl.when(order > 0)
        def _():
            remote(
                outs.at[order, k], in_ref.at[gy, k], x_send.at[order, k], x_recv.at[order, k], gx, to
            ).start()

        return carry

    lax.fori_loop(0, PLANE * CAP, one_piece, 0)
    local = pltpu.make_async_copy(outs.at[0], in_ref.at[gy], l_sem)
    local.start()

    for copy in copies + [p1, p2]:
        copy.wait_send()
    local.wait()

    def finish(i, carry):
        k = i % CAP
        order = i // CAP
        copy = remote(
            outs.at[order, k], in_ref.at[gy, k], x_send.at[order, k], x_recv.at[order, k], gx, partner_of(order)
        )
        copy.wait_send()
        copy.wait_recv()
        return carry

    def partner_of(order):
        return (y + order // SIDE) % SIDE * SIDE + (x + order % SIDE) % SIDE

    lax.fori_loop(CAP, PLANE * CAP, finish, 0)


def exchange(matrix_rows, tile_owner, tile_slot, slots):
    width = matrix_rows.shape[1]
    count = tile_owner.shape[0]
    lower_i, lower_j = np.tril_indices(TILE_COUNT)
    code = jnp.asarray(lower_i * TILE_COUNT + lower_j, jnp.int32).reshape(1, count)
    smem = pl.BlockSpec(memory_space=pltpu.SMEM)
    vmem = pl.BlockSpec(memory_space=pltpu.VMEM)
    dma = pltpu.SemaphoreType.DMA
    return pl.pallas_call(
        exchange_kernel,
        out_shape=(
            jax.ShapeDtypeStruct((PLANE, CAP, 2, CHUNK, CHUNK), jnp.float32),
            jax.ShapeDtypeStruct((slots,), jnp.int32),
        ),
        in_specs=[smem, vmem, vmem, vmem, vmem],
        out_specs=(pl.BlockSpec(memory_space=pl.ANY), smem),
        scratch_shapes=[
            pltpu.VMEM((HALF_TILES, TILE, width), jnp.float32),
            pltpu.VMEM((HALF_TILES, TILE, width), jnp.bfloat16),
            pltpu.VMEM((HALF_TILES, TILE, width), jnp.bfloat16),
            pltpu.VMEM((4, CHUNK, width), jnp.float32),
            pltpu.VMEM((STEPS, CHUNK, width), jnp.bfloat16),
            pltpu.VMEM((STEPS, CHUNK, width), jnp.bfloat16),
            pltpu.VMEM((PLANE, CAP, 2, CHUNK, CHUNK), jnp.float32),
            pltpu.SMEM((ENTRIES,), jnp.int32),
            pltpu.SMEM((ENTRIES,), jnp.int32),
            pltpu.SMEM((PLANE * CAP,), jnp.int32),
            pltpu.SMEM((slots,), jnp.int32),
            dma((2, 2)), dma((2, 2)), dma((2,)), dma((2,)),
            dma((4, 2, 2)), dma((4, 2, 2)), dma((4, 2)), dma((4, 2)),
            dma((2,)), dma((2,)), dma((2,)), dma((2,)),
            dma((PLANE, CAP)), dma((PLANE, CAP)), dma(()),
        ],
        compiler_params=pltpu.CompilerParams(
            collective_id=0, has_side_effects=True, vmem_limit_bytes=48 * 1024 * 1024
        ),
        name="exchange",
    )(tile_owner, tile_owner.reshape(1, count), tile_slot.reshape(1, count), code, matrix_rows)


def assemble_kernel(table, in_ref, out_ref, tiles, in_sem, out_sem):
    slots = tiles.shape[0]

    def pieces(q, act):
        entry = table[q]
        across = entry % 4 == 1
        source = entry // 4 % HALF_TILES * 2
        rank = entry // 32
        for h in range(2):
            for c in range(2):
                row = pl.multiple_of(jnp.where(across, h, c) * CHUNK, CHUNK)
                col = pl.multiple_of(jnp.where(across, c, h) * CHUNK, CHUNK)
                act(pltpu.make_async_copy(
                    in_ref.at[source + h, rank, c],
                    tiles.at[q, pl.ds(row, CHUNK), pl.ds(col, CHUNK)],
                    in_sem.at[q, 2 * h + c],
                ))

    def fetch(q, carry):
        present = table[q] % 4 > 0

        @pl.when(present)
        def _():
            pieces(q, lambda copy: copy.start())

        @pl.when(jnp.logical_not(present))
        def _():
            tiles[q] = jnp.zeros((TILE, TILE), jnp.float32)

        return carry

    def put(q, carry):
        @pl.when(table[q] % 4 > 0)
        def _():
            pieces(q, lambda copy: copy.wait())

        pltpu.make_async_copy(tiles.at[q], out_ref.at[q], out_sem.at[q]).start()
        return carry

    def finish(q, carry):
        pltpu.make_async_copy(tiles.at[q], out_ref.at[q], out_sem.at[q]).wait()
        return carry

    lax.fori_loop(0, slots, fetch, 0)
    lax.fori_loop(0, slots, put, 0)
    lax.fori_loop(0, slots, finish, 0)


def assemble(table, incoming):
    slots = table.shape[0]
    return pl.pallas_call(
        assemble_kernel,
        out_shape=jax.ShapeDtypeStruct((slots, TILE, TILE), jnp.float32),
        in_specs=[pl.BlockSpec(memory_space=pltpu.SMEM), pl.BlockSpec(memory_space=pl.ANY)],
        out_specs=pl.BlockSpec(memory_space=pl.ANY),
        scratch_shapes=[
            pltpu.VMEM((slots, TILE, TILE), jnp.float32),
            pltpu.SemaphoreType.DMA((slots, 4)),
            pltpu.SemaphoreType.DMA((slots,)),
        ],
        name="assemble",
    )(table, incoming)


def per_device(matrix_rows, tile_owner, tile_slot):
    devices = GROUPS * PLANE
    slots = (tile_owner.shape[0] + devices - 1) // devices
    incoming, table = exchange(matrix_rows, tile_owner, tile_slot, slots)
    return assemble(table, incoming)


def solution(mesh):
    placed = (P(("gx", "gy"), None), P(), P())
    return jax.shard_map(
        per_device,
        mesh=mesh,
        in_specs=placed,
        out_specs=P(("gx", "gy"), None, None),
        check_vma=False,
    )
```

time: 180 us -> 138 us (0.77); the launches traced: 178 us -> 138 us
  Pallas kernels: 171 us -> 133 us
  other arithmetic: 4.82 us -> 0 us
  local copies, waits for them, and re-layouts: 2.53 us -> 4.45 us
    pallas_call x1, Pallas kernels: 159 us -> 128 us  [exchange(): pl.pallas_call(exchange_kernel, out_shape=(jax.ShapeDtypeStruct((PLANE, C...]
    pallas_call x1, Pallas kernels: 11.8 us -> 5.51 us  [assemble(): pl.pallas_call(assemble_kernel, out_shape=jax.ShapeDtypeStruct((slots, TI...]
    unnamed x4 -> x8, local copies, waits for them, and re-layouts: 1.04 us -> 3.03 us
where the time goes in v2:
time: 138 us
  Pallas kernels  133 us (96%)
  local copies, waits for them, and re-layouts  4.45 us (3%)
    pallas_call x1, Pallas kernels, exchange(): pl.pallas_call(exchange_kernel, out_shape=(jax.ShapeDtypeStruct((PLANE, C...  128 us
    pallas_call x1, Pallas kernels, assemble(): pl.pallas_call(assemble_kernel, out_shape=jax.ShapeDtypeStruct((slots, TI...  5.51 us
    unnamed x8, local copies, waits for them, and re-layouts  3.03 us

profile of v2, /device:TPU:1, one launch (start us, length us, event | category | flops | bytes accessed | tf_op | source)
XLA Modules:
  0.0 137.9 jit_solution(2767610279235776618)
XLA Ops:
  0.0 0.7 reshape.10.slot_ref
  0.7 0.7 reshape.9.owner_ref
  1.4 0.0 copy-start
  1.4 1.0 copy-done
  2.5 0.0 copy-start.1
  2.5 0.7 copy-done.1
  3.2 0.0 copy-start.2
  3.2 0.7 copy-done.2
  3.9 127.9 %exchange.1 = (f32[16,3,2,128,128]{4,3,2,1,0:T(8,128)}, s32[17]{0:T(128)S(1)}) custom-call(s32[2080]{0:T(1024)S(1)} %copy-done.1, s32[1,2080]{1,0:T(1,128)S(1)} %reshape.9.owner_ref, s32[1,2080]{1,0:T(1,128)S(1)} %reshape.10.slot_ref, s32[1,2080]{1,0:T(1,128)S(1)} %copy-done.2, f32[128,1024]{1,0:T(8,128)S(1)} %copy-done), custom_call_target="tpu_custom_call" | custom-call | tf_op jit(solution)/shard_map/exchange/pallas_call | solution.py:361
  131.8 0.0 copy-start.3
  131.8 0.6 copy-done.3
  132.4 5.5 %assemble.1 = f32[17,256,256]{2,1,0:T(8,128)} custom-call(s32[17]{0:T(128)} %copy-done.3, f32[16,3,2,128,128]{4,3,2,1,0:T(8,128)} %get-tuple-element.8.in_ref), custom_call_target="tpu_custom_call" | custom-call | tf_op jit(solution)/shard_map/assemble/pallas_call | solution.py:443
Async XLA Ops:
  1.4 1.0 copy-start
  2.5 0.7 copy-start.1
  3.2 0.7 copy-start.2
  131.8 0.6 copy-start.3

commit v3 on v2

--- a/solution.py
+++ b/solution.py
@@ -18,10 +18,9 @@
 TILE = 256
 TILE_COUNT = 64
 ENTRIES = 33
-ORDER = (
-    (2, 2), (1, 0), (3, 0), (0, 2), (1, 1), (3, 3), (2, 0), (0, 1),
-    (0, 3), (1, 2), (3, 2), (1, 3), (3, 1), (2, 1), (2, 3), (0, 0),
-)
+ORDER = ((3, 2), (0, 1), (1, 1), (0, 2), (3, 3), (0, 3), (1, 0), (0, 0))
+SERVED = len(ORDER)
+PIECES = 2 * SERVED
 
 
 def entry_of(e, gx, r):
@@ -52,10 +51,11 @@
 
 
 def exchange_kernel(
-    owner_smem, owner_ref, slot_ref, code_ref, a_ref, in_ref, table_ref,
-    g, ghi, glo, rf, rhi, rlo, outs, target_tab, entry_tab, send_tab, found_tab,
+    owner_smem, owner_any, slot_any, code_any, a_any, in_ref, table_ref,
+    a_ref, owner_ref, slot_ref, code_ref,
+    g, ghi, glo, rf, qf, stage, rhi, rlo, outs, target_tab, entry_tab, send_tab, found_tab,
     a1_send, a1_recv, a2_send, a2_recv, b1_send, b1_recv, b2_send, b2_recv,
-    z_send, z_recv, p_send, p_recv, x_send, x_recv, l_sem,
+    z_send, z_recv, p_send, p_recv, q_send, q_recv, x_send, x_recv, l_sem,
 ):
     gx = lax.axis_index("gx")
     gy = lax.axis_index("gy")
@@ -73,23 +73,36 @@
     ahead = (gx + 2) % GROUPS
     behind = (gx + 6) % GROUPS
     partner = gx + 1 - 2 * core
+    crossed = (gx + 7 + 2 * core) % GROUPS
+    after = (gx + 1) % GROUPS
+
+    loads = [
+        pltpu.make_async_copy(src, dst, l_sem.at[n])
+        for n, (src, dst) in enumerate(
+            ((a_any, a_ref), (owner_any, owner_ref), (slot_any, slot_ref), (code_any, code_ref))
+        )
+    ]
+    for load in loads:
+        load.start()
 
     barrier = pltpu.get_barrier_semaphore()
-
-    def greet(i, carry):
+    for du, dv in ((1, 0), (3, 0), (0, 1), (0, 3)):
         pl.semaphore_signal(
-            barrier, inc=1, device_id={"gx": gx, "gy": (gy + i) % PLANE}, device_id_type=MESH
+            barrier, inc=1, device_id={"gx": gx, "gy": at(du, dv)}, device_id_type=MESH
         )
-        return carry
-
-    lax.fori_loop(1, PLANE, greet, 0)
-    for other in (ahead, behind, partner):
+    for other in (ahead, behind, partner, crossed):
         pl.semaphore_signal(barrier, inc=1, device_id={"gx": other, "gy": gy}, device_id_type=MESH)
-    pl.semaphore_wait(barrier, PLANE + 2)
+    loads[0].wait()
+    pl.semaphore_wait(barrier, 8)
+
+    def rows_of(c, h, size):
+        return pl.ds(pl.multiple_of(c % 2 * CHUNK + h * HALF, HALF), size)
 
     def half(c, h):
-        start = pl.multiple_of(c % 2 * CHUNK + h * HALF, HALF)
-        return g.at[c // 2, pl.ds(start, HALF)]
+        return g.at[c // 2, rows_of(c, h, HALF)]
+
+    def whole(c):
+        return g.at[c // 2, rows_of(c, 0, CHUNK)]
 
     def own_half(h):
         return a_ref.at[pl.ds(h * HALF, HALF)]
@@ -133,66 +146,113 @@
         )
         for d in (0, 1)
     ] for n, du in enumerate(offs)]
-    z1 = remote(a_ref, rf.at[1], z_send.at[0], z_recv.at[0], ahead, gy)
-    z2 = remote(rf.at[1], rf.at[3], z_send.at[1], z_recv.at[1], ahead, gy)
+
+    def along_z(n, src, dst, to):
+        return remote(src, dst, z_send.at[n], z_recv.at[n], to, gy)
+
+    z_near = along_z(0, a_ref, rf.at[1], ahead)
+    z_back = along_z(1, a_ref, stage.at[0], behind)
+    z_far = along_z(2, stage.at[0], rf.at[3], behind)
+
+    def along_q(n, src, dst, to):
+        return remote(src, dst, q_send.at[n], q_recv.at[n], to, gy)
+
+    opposite = at(2, 0)
+    q_near = along_q(1, whole(opposite), qf.at[1], ahead)
+    q_back = along_q(4, whole(opposite), stage.at[1], behind)
+    q_far = along_q(3, stage.at[1], qf.at[3], behind)
+    q_next = along_q(0, whole(at(0, 2)), qf.at[0], after)
+    q_third = along_q(2, qf.at[0], qf.at[2], ahead)
+
+    def to_partner(n, src, dst):
+        return remote(src, rf.at[dst], p_send.at[n], p_recv.at[n], partner, gy)
+
     for p in (0, 1):
         for d in (0, 1):
             start(a1[d][p])
-    start(z1)
+    start(z_near)
+    start(z_back)
     for p in (0, 1):
         for d in (0, 1):
             start(b1[0][d][p])
 
+    @pl.when(core == 0)
+    def _():
+        to_partner(0, a_ref, 0).start()
+
+    def split(value):
+        high = value.astype(jnp.bfloat16)
+        return high, (value - high.astype(jnp.float32)).astype(jnp.bfloat16)
+
     def split_g(c):
         block = c // 2
-        rows = pl.ds(pl.multiple_of(c % 2 * CHUNK, CHUNK), CHUNK)
-        value = g[block, rows, :]
-        high = value.astype(jnp.bfloat16)
+        rows = rows_of(c, 0, CHUNK)
+        high, low = split(g[block, rows, :])
         ghi[block, rows, :] = high
-        glo[block, rows, :] = (value - high.astype(jnp.float32)).astype(jnp.bfloat16)
+        glo[block, rows, :] = low
 
     def split_r(n, value):
-        high = value.astype(jnp.bfloat16)
+        high, low = split(value)
         rhi[n] = high
-        rlo[n] = (value - high.astype(jnp.float32)).astype(jnp.bfloat16)
-
-    own_r = gy // 2
-    for e in range(ENTRIES):
-        s, col, valid, rowwise, row_tile, col_tile = entry_of(e, gx, own_r)
-        owner = owner_smem[row_tile * (row_tile + 1) // 2 + col_tile] % PLANE
-        target_tab[e] = owner if valid is None else jnp.where(valid, owner, -1)
-        diag = jnp.where(row_tile == col_tile, 2, 0)
-        entry_tab[e] = s * 32 + col * 4 + diag + jnp.where(rowwise, 1, 0)
-
-    def fill(to, carry):
+        rlo[n] = low
+
+    for cls, chunk in enumerate((gy, opposite)):
+        class_r = chunk // 2
+        for e in range(ENTRIES):
+            s, col, valid, rowwise, row_tile, col_tile = entry_of(e, gx, class_r)
+            owner = owner_smem[row_tile * (row_tile + 1) // 2 + col_tile] % PLANE
+            target_tab[cls * ENTRIES + e] = owner if valid is None else jnp.where(valid, owner, -1)
+            diag = jnp.where(row_tile == col_tile, 2, 0)
+            step = s + STEPS * cls
+            entry_tab[cls * ENTRIES + e] = step * 32 + col * 4 + diag + jnp.where(rowwise, 1, 0)
+
+    def served(n):
+        du = jnp.int32(0)
+        dv = jnp.int32(0)
+        for m, (one, two) in enumerate(ORDER):
+            du = jnp.where(n == m, one, du)
+            dv = jnp.where(n == m, two, dv)
+        return at(du, dv)
+
+    def fill(p, carry):
+        to = served(p // 2)
+        base = p % 2 * ENTRIES
         kept = [jnp.int32(0)] * CAP
         for e in range(ENTRIES):
-            hit = target_tab[e] == to
-            fresh = entry_tab[e]
+            hit = target_tab[base + e] == to
+            fresh = entry_tab[base + e]
             kept = [jnp.where(hit, b, a) for a, b in zip(kept, [fresh] + kept[:-1])]
         for k in range(CAP):
-            send_tab[to * CAP + k] = kept[k]
-        return carry
-
-    lax.fori_loop(0, PLANE, fill, 0)
+            send_tab[p * CAP + k] = kept[k]
+        return carry
+
+    lax.fori_loop(0, PIECES, fill, 0)
 
     split_r(0, a_ref[...])
-    block, rows = me // 2, pl.ds(pl.multiple_of(me % 2 * CHUNK, CHUNK), CHUNK)
+    block, rows = me // 2, rows_of(me, 0, CHUNK)
     ghi[block, rows, :] = rhi[0]
     glo[block, rows, :] = rlo[0]
 
     for d in (0, 1):
         a1[d][0].wait_recv()
         start(a2[d])
+    z_back.wait_recv()
+    start(z_far)
     for d in (0, 1):
         a1[d][1].wait_recv()
         for p in (0, 1):
             for e in (0, 1):
                 start(b1[1 + d][e][p])
         split_g(at(-1 + 2 * d, 0))
-
-    z1.wait_recv()
-    start(z2)
+    z_near.wait_recv()
+
+    @pl.when(core == 0)
+    def _():
+        to_partner(1, rf.at[1], 2).start()
+
+    @pl.when(core == 1)
+    def _():
+        to_partner(0, rf.at[1], 0).start()
 
     def forward_v(n):
         for d in (0, 1):
@@ -204,6 +264,28 @@
             b1[n][d][1].wait_recv()
             split_g(at(offs[n], -1 + 2 * d))
 
+    def take_far(n):
+        for d in (0, 1):
+            b2[n][d].wait_recv()
+        if n == 0:
+            start(q_next)
+        split_g(at(offs[n], 2))
+
+    forward_v(0)
+    for d in (0, 1):
+        a2[d].wait_recv()
+        start(b1[3][d][0])
+    for d in (0, 1):
+        start(b1[3][d][1])
+    start(q_near)
+    start(q_back)
+    split_g(opposite)
+    high, low = split(whole(opposite)[...])
+    rhi[STEPS] = high
+    rlo[STEPS] = low
+
+    for load in loads[1:]:
+        load.wait()
     mine = owner_ref[...] == gx * PLANE + gy
     slots = table_ref.shape[0]
 
@@ -239,124 +321,119 @@
         table_ref[q] = table_ref[q] + 32 * jnp.minimum(later, CAP - 1)
         return carry
 
-    forward_v(0)
-    for d in (0, 1):
-        a2[d].wait_recv()
-        start(b1[3][d][0])
-    for d in (0, 1):
-        start(b1[3][d][1])
-    split_g(at(2, 0))
-
-    @pl.when(core == 0)
-    def _():
-        remote(a_ref, rf.at[0], p_send.at[0], p_recv.at[0], partner, gy).start()
+    take_v(0)
+    take_far(0)
+    forward_v(1)
+    z_far.wait_recv()
 
     @pl.when(core == 1)
     def _():
-        remote(rf.at[1], rf.at[0], p_send.at[0], p_recv.at[0], partner, gy).start()
-
-    take_v(0)
+        to_partner(1, rf.at[3], 2).start()
+
+    q_back.wait_recv()
+    start(q_far)
     lax.fori_loop(0, slots, count, 0)
+    take_v(1)
     split_r(2, rf[1])
-    forward_v(1)
-    z2.wait_recv()
-
-    @pl.when(core == 0)
-    def _():
-        remote(rf.at[1], rf.at[2], p_send.at[1], p_recv.at[1], partner, gy).start()
-
-    @pl.when(core == 1)
-    def _():
-        remote(rf.at[3], rf.at[2], p_send.at[1], p_recv.at[1], partner, gy).start()
-
-    take_v(1)
+    forward_v(2)
+    q_next.wait_recv()
+    start(q_third)
     split_r(4, rf[3])
-    forward_v(2)
-    p1 = remote(a_ref, rf.at[0], p_send.at[0], p_recv.at[0], partner, gy)
-    p2 = remote(a_ref, rf.at[2], p_send.at[1], p_recv.at[1], partner, gy)
+    p1 = to_partner(0, a_ref, 0)
+    p2 = to_partner(1, a_ref, 2)
     p1.wait_recv()
     split_r(1, rf[0])
     take_v(2)
-    forward_v(3)
     p2.wait_recv()
     split_r(3, rf[2])
+    forward_v(3)
+    split_r(STEPS + 1, qf[0])
+    q_near.wait_recv()
+    split_r(STEPS + 2, qf[1])
+    take_far(1)
+    take_far(2)
     take_v(3)
-    for n in range(4):
-        for d in (0, 1):
-            b2[n][d].wait_recv()
-        split_g(at(offs[n], 2))
-
-    row_in = lax.broadcasted_iota(jnp.int32, (CHUNK, TILE), 0) + gy % 2 * CHUNK
+    q_far.wait_recv()
+    split_r(STEPS + 4, qf[3])
+    take_far(3)
+    q_third.wait_recv()
+    split_r(STEPS + 3, qf[2])
+
+    row_in = lax.broadcasted_iota(jnp.int32, (CHUNK, TILE), 0)
     col_in = lax.broadcasted_iota(jnp.int32, (CHUNK, TILE), 1)
-    upper = row_in < col_in
 
     def dot(p, q):
         return lax.dot_general(p, q, (((1,), (1,)), ((), ())), preferred_element_type=jnp.float32)
 
     def one_piece(i, carry):
-        k = i // PLANE
-        n = i % PLANE
-        first = jnp.int32(0)
-        second = jnp.int32(0)
-        for m, (one, two) in enumerate(ORDER):
-            first = jnp.where(n == m, one, first)
-            second = jnp.where(n == m, two, second)
-        dy = jnp.where(core == 0, first, second)
-        dx = jnp.where(core == 0, second, first)
-        to = (y + dy) % SIDE * SIDE + (x + dx) % SIDE
-        order = dy * SIDE + dx
-        entry = send_tab[to * CAP + k]
+        k = i // PIECES
+        p = i % PIECES
+        to = served(p // 2)
+        chunk = jnp.where(p % 2 == 0, gy, opposite)
+        entry = send_tab[p * CAP + k]
         s = entry // 32
         j = entry // 4 % HALF_TILES
         rh = rhi[s]
         gh = ghi[j]
         value = dot(rh, gh) + dot(rh, glo[j]) + dot(rlo[s], gh)
+        upper = row_in + chunk % 2 * CHUNK < col_in
         masked = jnp.logical_and(upper, entry // 2 % 2 > 0)
         value = jnp.where(masked, jnp.float32(0.0), value)
         rowwise = jnp.full((CHUNK, CHUNK), entry % 2, jnp.int32) > 0
         for c in range(2):
             part = value[:, c * CHUNK:(c + 1) * CHUNK]
-            outs[order, k, c] = jnp.where(rowwise, part, part.T)
-
-        @pl.when(order > 0)
+            outs[p, k, c] = jnp.where(rowwise, part, part.T)
+
+        @pl.when(p < PIECES - 2)
         def _():
             remote(
-                outs.at[order, k], in_ref.at[gy, k], x_send.at[order, k], x_recv.at[order, k], gx, to
+                outs.at[p, k], in_ref.at[chunk, k], x_send.at[p, k], x_recv.at[chunk, k], gx, to
             ).start()
 
         return carry
 
-    lax.fori_loop(0, PLANE * CAP, one_piece, 0)
-    local = pltpu.make_async_copy(outs.at[0], in_ref.at[gy], l_sem)
-    local.start()
-
+    lax.fori_loop(0, PIECES * CAP, one_piece, 0)
+    local = [
+        pltpu.make_async_copy(outs.at[PIECES - 2 + n], in_ref.at[c], l_sem.at[n])
+        for n, c in enumerate((gy, opposite))
+    ]
+    for copy in local:
+        copy.start()
     for copy in copies + [p1, p2]:
         copy.wait_send()
-    local.wait()
-
-    def finish(i, carry):
-        k = i % CAP
-        order = i // CAP
-        copy = remote(
-            outs.at[order, k], in_ref.at[gy, k], x_send.at[order, k], x_recv.at[order, k], gx, partner_of(order)
-        )
-        copy.wait_send()
-        copy.wait_recv()
-        return carry
-
-    def partner_of(order):
-        return (y + order // SIDE) % SIDE * SIDE + (x + order % SIDE) % SIDE
-
-    lax.fori_loop(CAP, PLANE * CAP, finish, 0)
+    for copy in local:
+        copy.wait()
+
+    def sent(i, carry):
+        remote(
+            outs.at[i // CAP, i % CAP], in_ref.at[0, 0], x_send.at[i // CAP, i % CAP], x_recv.at[0, 0], ahead, gy
+        ).wait_send()
+        return carry
+
+    lax.fori_loop(0, (PIECES - 2) * CAP, sent, 0)
+
+    def arrived(i, carry):
+        du = i // CAP // SIDE
+        chunk = at(du, i // CAP % SIDE)
+
+        @pl.when(jnp.logical_or(i // CAP % SIDE > 0, du % 2 > 0))
+        def _():
+            remote(
+                outs.at[0, 0], in_ref.at[chunk, i % CAP], x_send.at[0, 0], x_recv.at[chunk, i % CAP], ahead, gy
+            ).wait_recv()
+
+        return carry
+
+    lax.fori_loop(0, PLANE * CAP, arrived, 0)
 
 
 def exchange(matrix_rows, tile_owner, tile_slot, slots):
-    width = matrix_rows.shape[1]
+    rows, width = matrix_rows.shape
     count = tile_owner.shape[0]
     lower_i, lower_j = np.tril_indices(TILE_COUNT)
-    code = jnp.asarray(lower_i * TILE_COUNT + lower_j, jnp.int32).reshape(1, count)
+    code = jnp.asarray(lower_i * TILE_COUNT + lower_j, jnp.int32)
     smem = pl.BlockSpec(memory_space=pltpu.SMEM)
-    vmem = pl.BlockSpec(memory_space=pltpu.VMEM)
+    hbm = pl.BlockSpec(memory_space=pl.ANY)
     dma = pltpu.SemaphoreType.DMA
     return pl.pallas_call(
         exchange_kernel,
@@ -364,30 +441,36 @@
             jax.ShapeDtypeStruct((PLANE, CAP, 2, CHUNK, CHUNK), jnp.float32),
             jax.ShapeDtypeStruct((slots,), jnp.int32),
         ),
-        in_specs=[smem, vmem, vmem, vmem, vmem],
-        out_specs=(pl.BlockSpec(memory_space=pl.ANY), smem),
+        in_specs=[smem, hbm, hbm, hbm, hbm],
+        out_specs=(hbm, smem),
         scratch_shapes=[
+            pltpu.VMEM((rows, width), jnp.float32),
+            pltpu.VMEM((count,), jnp.int32),
+            pltpu.VMEM((count,), jnp.int32),
+            pltpu.VMEM((count,), jnp.int32),
             pltpu.VMEM((HALF_TILES, TILE, width), jnp.float32),
             pltpu.VMEM((HALF_TILES, TILE, width), jnp.bfloat16),
             pltpu.VMEM((HALF_TILES, TILE, width), jnp.bfloat16),
             pltpu.VMEM((4, CHUNK, width), jnp.float32),
-            pltpu.VMEM((STEPS, CHUNK, width), jnp.bfloat16),
-            pltpu.VMEM((STEPS, CHUNK, width), jnp.bfloat16),
-            pltpu.VMEM((PLANE, CAP, 2, CHUNK, CHUNK), jnp.float32),
-            pltpu.SMEM((ENTRIES,), jnp.int32),
-            pltpu.SMEM((ENTRIES,), jnp.int32),
-            pltpu.SMEM((PLANE * CAP,), jnp.int32),
+            pltpu.VMEM((4, CHUNK, width), jnp.float32),
+            pltpu.VMEM((2, CHUNK, width), jnp.float32),
+            pltpu.VMEM((2 * STEPS, CHUNK, width), jnp.bfloat16),
+            pltpu.VMEM((2 * STEPS, CHUNK, width), jnp.bfloat16),
+            pltpu.VMEM((PIECES, CAP, 2, CHUNK, CHUNK), jnp.float32),
+            pltpu.SMEM((2 * ENTRIES,), jnp.int32),
+            pltpu.SMEM((2 * ENTRIES,), jnp.int32),
+            pltpu.SMEM((PIECES * CAP,), jnp.int32),
             pltpu.SMEM((slots,), jnp.int32),
             dma((2, 2)), dma((2, 2)), dma((2,)), dma((2,)),
             dma((4, 2, 2)), dma((4, 2, 2)), dma((4, 2)), dma((4, 2)),
-            dma((2,)), dma((2,)), dma((2,)), dma((2,)),
-            dma((PLANE, CAP)), dma((PLANE, CAP)), dma(()),
+            dma((3,)), dma((3,)), dma((2,)), dma((2,)), dma((5,)), dma((5,)),
+            dma((PIECES, CAP)), dma((PLANE, CAP)), dma((4,)),
         ],
         compiler_params=pltpu.CompilerParams(
-            collective_id=0, has_side_effects=True, vmem_limit_bytes=48 * 1024 * 1024
+            collective_id=0, has_side_effects=True, vmem_limit_bytes=56 * 1024 * 1024
         ),
         name="exchange",
-    )(tile_owner, tile_owner.reshape(1, count), tile_slot.reshape(1, count), code, matrix_rows)
+    )(tile_owner, tile_owner, tile_slot, code, matrix_rows)
 
 
 def assemble_kernel(table, in_ref, out_ref, tiles, in_sem, out_sem):

time: 138 us -> 120 us (0.87)
  Pallas kernels: 133 us -> 120 us
  local copies, waits for them, and re-layouts: 4.45 us -> 0 us
    pallas_call x1, Pallas kernels: 128 us -> 114 us  [exchange(): pl.pallas_call(exchange_kernel, out_shape=(jax.ShapeDtypeStruct((PLANE, C...]
    unnamed x8 -> x0, local copies, waits for them, and re-layouts: 3.03 us -> none
    reshape x2 -> x0, local copies, waits for them, and re-layouts: 1.43 us -> none  [the longest x1 0.71 us: exchange(): tile_slot.reshape(1, count)]
where the time goes in v3:
time: 120 us
  Pallas kernels  120 us (100%)
    pallas_call x1, Pallas kernels, exchange(): pl.pallas_call(exchange_kernel, out_shape=(jax.ShapeDtypeStruct((PLANE, C...  114 us
    pallas_call x1, Pallas kernels, assemble(): pl.pallas_call(assemble_kernel, out_shape=jax.ShapeDtypeStruct((slots, TI...  5.71 us

profile of v3, /device:TPU:1, one launch (start us, length us, event | category | flops | bytes accessed | tf_op | source)
XLA Modules:
  0.0 119.9 jit_solution(7131444666338814112)
XLA Ops:
  0.0 114.2 %exchange.1 = (f32[16,3,2,128,128]{4,3,2,1,0:T(8,128)}, s32[17]{0:T(128)}) custom-call(s32[2080]{0:T(1024)} %owner_any.1, s32[2080]{0:T(1024)} %owner_any.1, s32[2080]{0:T(1024)} %slot_any.1, s32[2080]{0:T(1024)} %constant.2.clone.code_any, f32[128,1024]{1,0:T(8,128)} %a_any.1), custom_call_target="tpu_custom_call" | custom-call | tf_op jit(solution)/shard_map/exchange/pallas_call | solution.py:438
  114.2 5.7 %assemble.1 = f32[17,256,256]{2,1,0:T(8,128)} custom-call(s32[17]{0:T(128)} %get-tuple-element.7.table, f32[16,3,2,128,128]{4,3,2,1,0:T(8,128)} %get-tuple-element.8.in_ref), custom_call_target="tpu_custom_call" | custom-call | tf_op jit(solution)/shard_map/assemble/pallas_call | solution.py:526

commit v4 on v3

--- a/solution.py
+++ b/solution.py
@@ -18,7 +18,7 @@
 TILE = 256
 TILE_COUNT = 64
 ENTRIES = 33
-ORDER = ((3, 2), (0, 1), (1, 1), (0, 2), (3, 3), (0, 3), (1, 0), (0, 0))
+ORDER = ((2, 0), (0, 1), (1, 9), (0, 3), (3, 9), (1, 0), (3, 0), (0, 0))
 SERVED = len(ORDER)
 PIECES = 2 * SERVED
 
@@ -73,8 +73,6 @@
     ahead = (gx + 2) % GROUPS
     behind = (gx + 6) % GROUPS
     partner = gx + 1 - 2 * core
-    crossed = (gx + 7 + 2 * core) % GROUPS
-    after = (gx + 1) % GROUPS
 
     loads = [
         pltpu.make_async_copy(src, dst, l_sem.at[n])
@@ -90,10 +88,10 @@
         pl.semaphore_signal(
             barrier, inc=1, device_id={"gx": gx, "gy": at(du, dv)}, device_id_type=MESH
         )
-    for other in (ahead, behind, partner, crossed):
+    for other in (ahead, behind, partner):
         pl.semaphore_signal(barrier, inc=1, device_id={"gx": other, "gy": gy}, device_id_type=MESH)
     loads[0].wait()
-    pl.semaphore_wait(barrier, 8)
+    pl.semaphore_wait(barrier, 7)
 
     def rows_of(c, h, size):
         return pl.ds(pl.multiple_of(c % 2 * CHUNK + h * HALF, HALF), size)
@@ -157,28 +155,25 @@
     def along_q(n, src, dst, to):
         return remote(src, dst, q_send.at[n], q_recv.at[n], to, gy)
 
-    opposite = at(2, 0)
-    q_near = along_q(1, whole(opposite), qf.at[1], ahead)
-    q_back = along_q(4, whole(opposite), stage.at[1], behind)
-    q_far = along_q(3, stage.at[1], qf.at[3], behind)
-    q_next = along_q(0, whole(at(0, 2)), qf.at[0], after)
-    q_third = along_q(2, qf.at[0], qf.at[2], ahead)
+    opposite = at(2, 2)
+    q_near = along_q(0, whole(opposite), qf.at[1], ahead)
+    q_back = along_q(1, whole(opposite), stage.at[1], behind)
+    q_far = along_q(2, stage.at[1], qf.at[3], behind)
 
     def to_partner(n, src, dst):
-        return remote(src, rf.at[dst], p_send.at[n], p_recv.at[n], partner, gy)
+        return remote(src, dst, p_send.at[n], p_recv.at[n], partner, gy)
+
+    p_of = [to_partner(n, a_ref, dst) for n, dst in enumerate((rf.at[0], rf.at[2], qf.at[0], qf.at[2]))]
 
     for p in (0, 1):
         for d in (0, 1):
             start(a1[d][p])
     start(z_near)
     start(z_back)
-    for p in (0, 1):
-        for d in (0, 1):
-            start(b1[0][d][p])
 
     @pl.when(core == 0)
     def _():
-        to_partner(0, a_ref, 0).start()
+        to_partner(0, a_ref, rf.at[0]).start()
 
     def split(value):
         high = value.astype(jnp.bfloat16)
@@ -206,16 +201,17 @@
             step = s + STEPS * cls
             entry_tab[cls * ENTRIES + e] = step * 32 + col * 4 + diag + jnp.where(rowwise, 1, 0)
 
-    def served(n):
+    def served(n, cls):
         du = jnp.int32(0)
         dv = jnp.int32(0)
         for m, (one, two) in enumerate(ORDER):
             du = jnp.where(n == m, one, du)
             dv = jnp.where(n == m, two, dv)
-        return at(du, dv)
+        side = jnp.where((u + 2 * cls) % SIDE < 2, 1, 3)
+        return at(du, jnp.where(dv == 9, side, dv))
 
     def fill(p, carry):
-        to = served(p // 2)
+        to = served(p // 2, p % 2)
         base = p % 2 * ENTRIES
         kept = [jnp.int32(0)] * CAP
         for e in range(ENTRIES):
@@ -226,8 +222,6 @@
             send_tab[p * CAP + k] = kept[k]
         return carry
 
-    lax.fori_loop(0, PIECES, fill, 0)
-
     split_r(0, a_ref[...])
     block, rows = me // 2, rows_of(me, 0, CHUNK)
     ghi[block, rows, :] = rhi[0]
@@ -236,23 +230,16 @@
     for d in (0, 1):
         a1[d][0].wait_recv()
         start(a2[d])
-    z_back.wait_recv()
-    start(z_far)
+    for d in (0, 1):
+        start(b1[0][d][0])
     for d in (0, 1):
         a1[d][1].wait_recv()
-        for p in (0, 1):
-            for e in (0, 1):
-                start(b1[1 + d][e][p])
         split_g(at(-1 + 2 * d, 0))
-    z_near.wait_recv()
-
-    @pl.when(core == 0)
-    def _():
-        to_partner(1, rf.at[1], 2).start()
-
-    @pl.when(core == 1)
-    def _():
-        to_partner(0, rf.at[1], 0).start()
+    for d in (0, 1):
+        a2[d].wait_recv()
+        start(b1[3][d][0])
+    split_g(at(2, 0))
+    lax.fori_loop(0, PIECES, fill, 0)
 
     def forward_v(n):
         for d in (0, 1):
@@ -267,22 +254,39 @@
     def take_far(n):
         for d in (0, 1):
             b2[n][d].wait_recv()
-        if n == 0:
-            start(q_next)
         split_g(at(offs[n], 2))
 
+    forward_v(3)
     forward_v(0)
+    for n, p in ((1, 0), (2, 0), (3, 1), (0, 1)):
+        for d in (0, 1):
+            start(b1[n][d][p])
+    z_back.wait_recv()
+    start(z_far)
+    z_near.wait_recv()
+
+    @pl.when(core == 0)
+    def _():
+        to_partner(1, rf.at[1], rf.at[2]).start()
+
+    @pl.when(core == 1)
+    def _():
+        to_partner(0, rf.at[1], rf.at[0]).start()
+
     for d in (0, 1):
-        a2[d].wait_recv()
-        start(b1[3][d][0])
-    for d in (0, 1):
-        start(b1[3][d][1])
+        b2[3][d].wait_recv()
     start(q_near)
     start(q_back)
+
+    @pl.when(core == 0)
+    def _():
+        to_partner(2, whole(opposite), qf.at[0]).start()
+
     split_g(opposite)
     high, low = split(whole(opposite)[...])
     rhi[STEPS] = high
     rlo[STEPS] = low
+    split_r(2, rf[1])
 
     for load in loads[1:]:
         load.wait()
@@ -321,43 +325,54 @@
         table_ref[q] = table_ref[q] + 32 * jnp.minimum(later, CAP - 1)
         return carry
 
-    take_v(0)
-    take_far(0)
-    forward_v(1)
+    for n in (1, 2):
+        forward_v(n)
+    for n in (1, 2):
+        for d in (0, 1):
+            start(b1[n][d][1])
     z_far.wait_recv()
 
     @pl.when(core == 1)
     def _():
-        to_partner(1, rf.at[3], 2).start()
+        to_partner(1, rf.at[3], rf.at[2]).start()
 
     q_back.wait_recv()
     start(q_far)
+    q_near.wait_recv()
+
+    @pl.when(core == 0)
+    def _():
+        to_partner(3, qf.at[1], qf.at[2]).start()
+
+    @pl.when(core == 1)
+    def _():
+        to_partner(2, qf.at[1], qf.at[0]).start()
+
     lax.fori_loop(0, slots, count, 0)
-    take_v(1)
-    split_r(2, rf[1])
-    forward_v(2)
-    q_next.wait_recv()
-    start(q_third)
+    take_far(0)
     split_r(4, rf[3])
-    p1 = to_partner(0, a_ref, 0)
-    p2 = to_partner(1, a_ref, 2)
-    p1.wait_recv()
+    split_r(STEPS + 2, qf[1])
+    p_of[0].wait_recv()
     split_r(1, rf[0])
-    take_v(2)
-    p2.wait_recv()
+    p_of[1].wait_recv()
     split_r(3, rf[2])
-    forward_v(3)
+    take_v(3)
+    take_v(0)
+    p_of[2].wait_recv()
     split_r(STEPS + 1, qf[0])
-    q_near.wait_recv()
-    split_r(STEPS + 2, qf[1])
+    q_far.wait_recv()
+
+    @pl.when(core == 1)
+    def _():
+        to_partner(3, qf.at[3], qf.at[2]).start()
+
+    split_r(STEPS + 4, qf[3])
     take_far(1)
     take_far(2)
-    take_v(3)
-    q_far.wait_recv()
-    split_r(STEPS + 4, qf[3])
-    take_far(3)
-    q_third.wait_recv()
+    p_of[3].wait_recv()
     split_r(STEPS + 3, qf[2])
+    take_v(1)
+    take_v(2)
 
     row_in = lax.broadcasted_iota(jnp.int32, (CHUNK, TILE), 0)
     col_in = lax.broadcasted_iota(jnp.int32, (CHUNK, TILE), 1)
@@ -368,7 +383,7 @@
     def one_piece(i, carry):
         k = i // PIECES
         p = i % PIECES
-        to = served(p // 2)
+        to = served(p // 2, p % 2)
         chunk = jnp.where(p % 2 == 0, gy, opposite)
         entry = send_tab[p * CAP + k]
         s = entry // 32
@@ -399,7 +414,7 @@
     ]
     for copy in local:
         copy.start()
-    for copy in copies + [p1, p2]:
+    for copy in copies + p_of:
         copy.wait_send()
     for copy in local:
         copy.wait()
@@ -414,9 +429,10 @@
 
     def arrived(i, carry):
         du = i // CAP // SIDE
-        chunk = at(du, i // CAP % SIDE)
-
-        @pl.when(jnp.logical_or(i // CAP % SIDE > 0, du % 2 > 0))
+        dv = i // CAP % SIDE
+        chunk = at(du, dv)
+
+        @pl.when(jnp.logical_or(du != dv, du % 2 > 0))
         def _():
             remote(
                 outs.at[0, 0], in_ref.at[chunk, i % CAP], x_send.at[0, 0], x_recv.at[chunk, i % CAP], ahead, gy
@@ -463,7 +479,7 @@
             pltpu.SMEM((slots,), jnp.int32),
             dma((2, 2)), dma((2, 2)), dma((2,)), dma((2,)),
             dma((4, 2, 2)), dma((4, 2, 2)), dma((4, 2)), dma((4, 2)),
-            dma((3,)), dma((3,)), dma((2,)), dma((2,)), dma((5,)), dma((5,)),
+            dma((3,)), dma((3,)), dma((4,)), dma((4,)), dma((3,)), dma((3,)),
             dma((PIECES, CAP)), dma((PLANE, CAP)), dma((4,)),
         ],
         compiler_params=pltpu.CompilerParams(

time: 120 us -> 114 us (0.950)
  Pallas kernels: 120 us -> 114 us
    pallas_call x1, Pallas kernels: 114 us -> 108 us  [exchange(): pl.pallas_call(exchange_kernel, out_shape=(jax.ShapeDtypeStruct((PLANE, C...]
where the time goes in v4:
time: 114 us
  Pallas kernels  114 us (100%)
    pallas_call x1, Pallas kernels, exchange(): pl.pallas_call(exchange_kernel, out_shape=(jax.ShapeDtypeStruct((PLANE, C...  108 us
    pallas_call x1, Pallas kernels, assemble(): pl.pallas_call(assemble_kernel, out_shape=jax.ShapeDtypeStruct((slots, TI...  5.51 us

profile of v4, /device:TPU:1, one launch (start us, length us, event | category | flops | bytes accessed | tf_op | source)
XLA Modules:
  0.0 113.7 jit_solution(17710996648754756078)
XLA Ops:
  0.0 108.2 %exchange.1 = (f32[16,3,2,128,128]{4,3,2,1,0:T(8,128)}, s32[17]{0:T(128)}) custom-call(s32[2080]{0:T(1024)} %owner_any.1, s32[2080]{0:T(1024)} %owner_any.1, s32[2080]{0:T(1024)} %slot_any.1, s32[2080]{0:T(1024)} %constant.2.clone.code_any, f32[128,1024]{1,0:T(8,128)} %a_any.1), custom_call_target="tpu_custom_call" | custom-call | tf_op jit(solution)/shard_map/exchange/pallas_call | solution.py:454
  108.2 5.5 %assemble.1 = f32[17,256,256]{2,1,0:T(8,128)} custom-call(s32[17]{0:T(128)} %get-tuple-element.7.table, f32[16,3,2,128,128]{4,3,2,1,0:T(8,128)} %get-tuple-element.8.in_ref), custom_call_target="tpu_custom_call" | custom-call | tf_op jit(solution)/shard_map/assemble/pallas_call | solution.py:542

commit v5 on v4

--- a/solution.py
+++ b/solution.py
@@ -53,7 +53,7 @@
 def exchange_kernel(
     owner_smem, owner_any, slot_any, code_any, a_any, in_ref, table_ref,
     a_ref, owner_ref, slot_ref, code_ref,
-    g, ghi, glo, rf, qf, stage, rhi, rlo, outs, target_tab, entry_tab, send_tab, found_tab,
+    g, ghi, glo, rf, qf, rhi, rlo, outs, target_tab, entry_tab, send_tab, found_tab,
     a1_send, a1_recv, a2_send, a2_recv, b1_send, b1_recv, b2_send, b2_recv,
     z_send, z_recv, p_send, p_recv, q_send, q_recv, x_send, x_recv, l_sem,
 ):
@@ -72,6 +72,7 @@
 
     ahead = (gx + 2) % GROUPS
     behind = (gx + 6) % GROUPS
+    beyond = (gx + 4) % GROUPS
     partner = gx + 1 - 2 * core
 
     loads = [
@@ -88,10 +89,10 @@
         pl.semaphore_signal(
             barrier, inc=1, device_id={"gx": gx, "gy": at(du, dv)}, device_id_type=MESH
         )
-    for other in (ahead, behind, partner):
+    for other in (ahead, behind, beyond, partner):
         pl.semaphore_signal(barrier, inc=1, device_id={"gx": other, "gy": gy}, device_id_type=MESH)
     loads[0].wait()
-    pl.semaphore_wait(barrier, 7)
+    pl.semaphore_wait(barrier, 8)
 
     def rows_of(c, h, size):
         return pl.ds(pl.multiple_of(c % 2 * CHUNK + h * HALF, HALF), size)
@@ -149,16 +150,14 @@
         return remote(src, dst, z_send.at[n], z_recv.at[n], to, gy)
 
     z_near = along_z(0, a_ref, rf.at[1], ahead)
-    z_back = along_z(1, a_ref, stage.at[0], behind)
-    z_far = along_z(2, stage.at[0], rf.at[3], behind)
+    z_far = along_z(1, a_ref, rf.at[3], beyond)
 
     def along_q(n, src, dst, to):
         return remote(src, dst, q_send.at[n], q_recv.at[n], to, gy)
 
     opposite = at(2, 2)
     q_near = along_q(0, whole(opposite), qf.at[1], ahead)
-    q_back = along_q(1, whole(opposite), stage.at[1], behind)
-    q_far = along_q(2, stage.at[1], qf.at[3], behind)
+    q_far = along_q(1, whole(opposite), qf.at[3], beyond)
 
     def to_partner(n, src, dst):
         return remote(src, dst, p_send.at[n], p_recv.at[n], partner, gy)
@@ -169,7 +168,7 @@
         for d in (0, 1):
             start(a1[d][p])
     start(z_near)
-    start(z_back)
+    start(z_far)
 
     @pl.when(core == 0)
     def _():
@@ -227,25 +226,6 @@
     ghi[block, rows, :] = rhi[0]
     glo[block, rows, :] = rlo[0]
 
-    for d in (0, 1):
-        a1[d][0].wait_recv()
-        start(a2[d])
-    for d in (0, 1):
-        start(b1[0][d][0])
-    for d in (0, 1):
-        a1[d][1].wait_recv()
-        split_g(at(-1 + 2 * d, 0))
-    for d in (0, 1):
-        a2[d].wait_recv()
-        start(b1[3][d][0])
-    split_g(at(2, 0))
-    lax.fori_loop(0, PIECES, fill, 0)
-
-    def forward_v(n):
-        for d in (0, 1):
-            b1[n][d][0].wait_recv()
-            start(b2[n][d])
-
     def take_v(n):
         for d in (0, 1):
             b1[n][d][1].wait_recv()
@@ -256,37 +236,66 @@
             b2[n][d].wait_recv()
         split_g(at(offs[n], 2))
 
-    forward_v(3)
-    forward_v(0)
-    for n, p in ((1, 0), (2, 0), (3, 1), (0, 1)):
-        for d in (0, 1):
-            start(b1[n][d][p])
-    z_back.wait_recv()
-    start(z_far)
-    z_near.wait_recv()
-
-    @pl.when(core == 0)
-    def _():
-        to_partner(1, rf.at[1], rf.at[2]).start()
-
-    @pl.when(core == 1)
-    def _():
-        to_partner(0, rf.at[1], rf.at[0]).start()
-
+    for d in (0, 1):
+        a1[d][0].wait_recv()
+        start(a2[d])
+    for d in (0, 1):
+        a1[d][1].wait_recv()
+        start(b1[0][d][0])
+    for d in (0, 1):
+        split_g(at(-1 + 2 * d, 0))
+    for d in (0, 1):
+        a2[d].wait_recv()
+        start(b1[3][d][0])
+    for d in (0, 1):
+        b1[0][d][0].wait_recv()
+        start(b1[0][d][1])
+    split_g(at(2, 0))
+    for d in (0, 1):
+        b1[3][d][0].wait_recv()
+        start(b2[3][d])
+    for d in (0, 1):
+        b1[0][d][1].wait_recv()
+        start(b2[0][d])
+        start(b1[1][d][0])
+        start(b1[2][d][0])
+    for d in (0, 1):
+        split_g(at(0, -1 + 2 * d))
     for d in (0, 1):
         b2[3][d].wait_recv()
     start(q_near)
-    start(q_back)
+    start(q_far)
 
     @pl.when(core == 0)
     def _():
         to_partner(2, whole(opposite), qf.at[0]).start()
 
+    for n in (3, 1, 2):
+        for d in (0, 1):
+            start(b1[n][d][1])
     split_g(opposite)
     high, low = split(whole(opposite)[...])
     rhi[STEPS] = high
     rlo[STEPS] = low
+    z_near.wait_recv()
+
+    @pl.when(core == 0)
+    def _():
+        to_partner(1, rf.at[1], rf.at[2]).start()
+
+    @pl.when(core == 1)
+    def _():
+        to_partner(0, rf.at[1], rf.at[0]).start()
+
     split_r(2, rf[1])
+    z_far.wait_recv()
+
+    @pl.when(core == 1)
+    def _():
+        to_partner(1, rf.at[3], rf.at[2]).start()
+
+    split_r(4, rf[3])
+    lax.fori_loop(0, PIECES, fill, 0)
 
     for load in loads[1:]:
         load.wait()
@@ -326,53 +335,42 @@
         return carry
 
     for n in (1, 2):
-        forward_v(n)
-    for n in (1, 2):
         for d in (0, 1):
-            start(b1[n][d][1])
-    z_far.wait_recv()
-
-    @pl.when(core == 1)
-    def _():
-        to_partner(1, rf.at[3], rf.at[2]).start()
-
-    q_back.wait_recv()
-    start(q_far)
-    q_near.wait_recv()
-
-    @pl.when(core == 0)
-    def _():
-        to_partner(3, qf.at[1], qf.at[2]).start()
-
-    @pl.when(core == 1)
-    def _():
-        to_partner(2, qf.at[1], qf.at[0]).start()
-
+            b1[n][d][0].wait_recv()
+            start(b2[n][d])
     lax.fori_loop(0, slots, count, 0)
     take_far(0)
-    split_r(4, rf[3])
-    split_r(STEPS + 2, qf[1])
     p_of[0].wait_recv()
     split_r(1, rf[0])
     p_of[1].wait_recv()
     split_r(3, rf[2])
     take_v(3)
-    take_v(0)
+    q_near.wait_recv()
+
+    @pl.when(core == 0)
+    def _():
+        to_partner(3, qf.at[1], qf.at[2]).start()
+
+    @pl.when(core == 1)
+    def _():
+        to_partner(2, qf.at[1], qf.at[0]).start()
+
+    split_r(STEPS + 2, qf[1])
+    take_v(1)
+    take_v(2)
     p_of[2].wait_recv()
     split_r(STEPS + 1, qf[0])
-    q_far.wait_recv()
-
-    @pl.when(core == 1)
-    def _():
-        to_partner(3, qf.at[3], qf.at[2]).start()
-
-    split_r(STEPS + 4, qf[3])
     take_far(1)
     take_far(2)
+    q_far.wait_recv()
+
+    @pl.when(core == 1)
+    def _():
+        to_partner(3, qf.at[3], qf.at[2]).start()
+
+    split_r(STEPS + 4, qf[3])
     p_of[3].wait_recv()
     split_r(STEPS + 3, qf[2])
-    take_v(1)
-    take_v(2)
 
     row_in = lax.broadcasted_iota(jnp.int32, (CHUNK, TILE), 0)
     col_in = lax.broadcasted_iota(jnp.int32, (CHUNK, TILE), 1)
@@ -469,7 +467,6 @@
             pltpu.VMEM((HALF_TILES, TILE, width), jnp.bfloat16),
             pltpu.VMEM((4, CHUNK, width), jnp.float32),
             pltpu.VMEM((4, CHUNK, width), jnp.float32),
-            pltpu.VMEM((2, CHUNK, width), jnp.float32),
             pltpu.VMEM((2 * STEPS, CHUNK, width), jnp.bfloat16),
             pltpu.VMEM((2 * STEPS, CHUNK, width), jnp.bfloat16),
             pltpu.VMEM((PIECES, CAP, 2, CHUNK, CHUNK), jnp.float32),
@@ -479,7 +476,7 @@
             pltpu.SMEM((slots,), jnp.int32),
             dma((2, 2)), dma((2, 2)), dma((2,)), dma((2,)),
             dma((4, 2, 2)), dma((4, 2, 2)), dma((4, 2)), dma((4, 2)),
-            dma((3,)), dma((3,)), dma((4,)), dma((4,)), dma((3,)), dma((3,)),
+            dma((2,)), dma((2,)), dma((4,)), dma((4,)), dma((2,)), dma((2,)),
             dma((PIECES, CAP)), dma((PLANE, CAP)), dma((4,)),
         ],
         compiler_params=pltpu.CompilerParams(

time: 114 us -> 112 us (0.982)
  Pallas kernels: 114 us -> 112 us
    pallas_call x1, Pallas kernels: 108 us -> 106 us  [exchange(): pl.pallas_call(exchange_kernel, out_shape=(jax.ShapeDtypeStruct((PLANE, C...]
where the time goes in v5:
time: 112 us
  Pallas kernels  112 us (100%)
    pallas_call x1, Pallas kernels, exchange(): pl.pallas_call(exchange_kernel, out_shape=(jax.ShapeDtypeStruct((PLANE, C...  106 us
    pallas_call x1, Pallas kernels, assemble(): pl.pallas_call(assemble_kernel, out_shape=jax.ShapeDtypeStruct((slots, TI...  5.51 us

profile of v5, /device:TPU:1, one launch (start us, length us, event | category | flops | bytes accessed | tf_op | source)
XLA Modules:
  0.0 112.0 jit_solution(5125848472989315025)
XLA Ops:
  0.0 106.4 %exchange.1 = (f32[16,3,2,128,128]{4,3,2,1,0:T(8,128)}, s32[17]{0:T(128)}) custom-call(s32[2080]{0:T(1024)} %owner_any.1, s32[2080]{0:T(1024)} %owner_any.1, s32[2080]{0:T(1024)} %slot_any.1, s32[2080]{0:T(1024)} %constant.2.clone.code_any, f32[128,1024]{1,0:T(8,128)} %a_any.1), custom_call_target="tpu_custom_call" | custom-call | tf_op jit(solution)/shard_map/exchange/pallas_call | solution.py:452
  106.5 5.5 %assemble.1 = f32[17,256,256]{2,1,0:T(8,128)} custom-call(s32[17]{0:T(128)} %get-tuple-element.7.table, f32[16,3,2,128,128]{4,3,2,1,0:T(8,128)} %get-tuple-element.8.in_ref), custom_call_target="tpu_custom_call" | custom-call | tf_op jit(solution)/shard_map/assemble/pallas_call | solution.py:539

commit v6 on v5

--- a/solution.py
+++ b/solution.py
@@ -167,6 +167,9 @@
     for p in (0, 1):
         for d in (0, 1):
             start(a1[d][p])
+    for p in (0, 1):
+        for d in (0, 1):
+            start(b1[0][d][p])
     start(z_near)
     start(z_far)
 
@@ -221,81 +224,11 @@
             send_tab[p * CAP + k] = kept[k]
         return carry
 
+    lax.fori_loop(0, PIECES, fill, 0)
     split_r(0, a_ref[...])
     block, rows = me // 2, rows_of(me, 0, CHUNK)
     ghi[block, rows, :] = rhi[0]
     glo[block, rows, :] = rlo[0]
-
-    def take_v(n):
-        for d in (0, 1):
-            b1[n][d][1].wait_recv()
-            split_g(at(offs[n], -1 + 2 * d))
-
-    def take_far(n):
-        for d in (0, 1):
-            b2[n][d].wait_recv()
-        split_g(at(offs[n], 2))
-
-    for d in (0, 1):
-        a1[d][0].wait_recv()
-        start(a2[d])
-    for d in (0, 1):
-        a1[d][1].wait_recv()
-        start(b1[0][d][0])
-    for d in (0, 1):
-        split_g(at(-1 + 2 * d, 0))
-    for d in (0, 1):
-        a2[d].wait_recv()
-        start(b1[3][d][0])
-    for d in (0, 1):
-        b1[0][d][0].wait_recv()
-        start(b1[0][d][1])
-    split_g(at(2, 0))
-    for d in (0, 1):
-        b1[3][d][0].wait_recv()
-        start(b2[3][d])
-    for d in (0, 1):
-        b1[0][d][1].wait_recv()
-        start(b2[0][d])
-        start(b1[1][d][0])
-        start(b1[2][d][0])
-    for d in (0, 1):
-        split_g(at(0, -1 + 2 * d))
-    for d in (0, 1):
-        b2[3][d].wait_recv()
-    start(q_near)
-    start(q_far)
-
-    @pl.when(core == 0)
-    def _():
-        to_partner(2, whole(opposite), qf.at[0]).start()
-
-    for n in (3, 1, 2):
-        for d in (0, 1):
-            start(b1[n][d][1])
-    split_g(opposite)
-    high, low = split(whole(opposite)[...])
-    rhi[STEPS] = high
-    rlo[STEPS] = low
-    z_near.wait_recv()
-
-    @pl.when(core == 0)
-    def _():
-        to_partner(1, rf.at[1], rf.at[2]).start()
-
-    @pl.when(core == 1)
-    def _():
-        to_partner(0, rf.at[1], rf.at[0]).start()
-
-    split_r(2, rf[1])
-    z_far.wait_recv()
-
-    @pl.when(core == 1)
-    def _():
-        to_partner(1, rf.at[3], rf.at[2]).start()
-
-    split_r(4, rf[3])
-    lax.fori_loop(0, PIECES, fill, 0)
 
     for load in loads[1:]:
         load.wait()
@@ -322,8 +255,6 @@
         table_ref[q] = jnp.where(found >= 0, jnp.where(rowwise, 1, 2), 0) + class_r * 4
         return carry
 
-    lax.fori_loop(0, slots, find, 0)
-
     def count(q, carry):
         own = found_tab[q]
         later = jnp.int32(0)
@@ -334,43 +265,91 @@
         table_ref[q] = table_ref[q] + 32 * jnp.minimum(later, CAP - 1)
         return carry
 
-    for n in (1, 2):
+    def take_v(n):
         for d in (0, 1):
-            b1[n][d][0].wait_recv()
-            start(b2[n][d])
-    lax.fori_loop(0, slots, count, 0)
+            b1[n][d][1].wait_recv()
+            split_g(at(offs[n], -1 + 2 * d))
+
+    def take_far(n):
+        for d in (0, 1):
+            b2[n][d].wait_recv()
+        split_g(at(offs[n], 2))
+
+    for d in (0, 1):
+        a1[d][0].wait_recv()
+        start(a2[d])
+    for d in (0, 1):
+        a1[d][1].wait_recv()
+    for p in (0, 1):
+        for d in (0, 1):
+            start(b1[1][d][p])
+    for d in (0, 1):
+        split_g(at(-1 + 2 * d, 0))
+    for d in (0, 1):
+        a2[d].wait_recv()
+        start(b1[3][d][0])
+    for d in (0, 1):
+        start(b1[3][d][1])
+    for d in (0, 1):
+        b1[0][d][0].wait_recv()
+        start(b2[0][d])
+    split_g(at(2, 0))
+    for d in (0, 1):
+        b1[3][d][0].wait_recv()
+        start(b2[3][d])
+    for p in (0, 1):
+        for d in (0, 1):
+            start(b1[2][d][p])
+    for d in (0, 1):
+        b1[1][d][0].wait_recv()
+        start(b2[1][d])
+    z_near.wait_recv()
+
+    @pl.when(core == 0)
+    def _():
+        to_partner(1, rf.at[1], rf.at[2]).start()
+
+    @pl.when(core == 1)
+    def _():
+        to_partner(0, rf.at[1], rf.at[0]).start()
+
+    take_v(0)
+    split_r(2, rf[1])
+    z_far.wait_recv()
+
+    @pl.when(core == 1)
+    def _():
+        to_partner(1, rf.at[3], rf.at[2]).start()
+
+    split_r(4, rf[3])
     take_far(0)
+    for d in (0, 1):
+        b2[3][d].wait_recv()
+    start(q_near)
+    start(q_far)
+
+    @pl.when(core == 0)
+    def _():
+        to_partner(2, whole(opposite), qf.at[0]).start()
+
+    for d in (0, 1):
+        b1[2][d][0].wait_recv()
+        start(b2[2][d])
+    split_g(opposite)
+    high, low = split(whole(opposite)[...])
+    rhi[STEPS] = high
+    rlo[STEPS] = low
+    lax.fori_loop(0, slots, find, 0)
+    take_v(1)
+    take_v(3)
     p_of[0].wait_recv()
     split_r(1, rf[0])
     p_of[1].wait_recv()
     split_r(3, rf[2])
-    take_v(3)
-    q_near.wait_recv()
-
-    @pl.when(core == 0)
-    def _():
-        to_partner(3, qf.at[1], qf.at[2]).start()
-
-    @pl.when(core == 1)
-    def _():
-        to_partner(2, qf.at[1], qf.at[0]).start()
-
-    split_r(STEPS + 2, qf[1])
-    take_v(1)
+    lax.fori_loop(0, slots, count, 0)
     take_v(2)
-    p_of[2].wait_recv()
-    split_r(STEPS + 1, qf[0])
     take_far(1)
     take_far(2)
-    q_far.wait_recv()
-
-    @pl.when(core == 1)
-    def _():
-        to_partner(3, qf.at[3], qf.at[2]).start()
-
-    split_r(STEPS + 4, qf[3])
-    p_of[3].wait_recv()
-    split_r(STEPS + 3, qf[2])
 
     row_in = lax.broadcasted_iota(jnp.int32, (CHUNK, TILE), 0)
     col_in = lax.broadcasted_iota(jnp.int32, (CHUNK, TILE), 1)
@@ -379,8 +358,8 @@
         return lax.dot_general(p, q, (((1,), (1,)), ((), ())), preferred_element_type=jnp.float32)
 
     def one_piece(i, carry):
-        k = i // PIECES
-        p = i % PIECES
+        k = i // SERVED % CAP
+        p = i % SERVED * 2 + i // (SERVED * CAP)
         to = served(p // 2, p % 2)
         chunk = jnp.where(p % 2 == 0, gy, opposite)
         entry = send_tab[p * CAP + k]
@@ -405,7 +384,31 @@
 
         return carry
 
-    lax.fori_loop(0, PIECES * CAP, one_piece, 0)
+    lax.fori_loop(0, SERVED, one_piece, 0)
+    q_near.wait_recv()
+
+    @pl.when(core == 0)
+    def _():
+        to_partner(3, qf.at[1], qf.at[2]).start()
+
+    @pl.when(core == 1)
+    def _():
+        to_partner(2, qf.at[1], qf.at[0]).start()
+
+    split_r(STEPS + 2, qf[1])
+    lax.fori_loop(SERVED, SERVED * CAP, one_piece, 0)
+    q_far.wait_recv()
+
+    @pl.when(core == 1)
+    def _():
+        to_partner(3, qf.at[3], qf.at[2]).start()
+
+    split_r(STEPS + 4, qf[3])
+    p_of[2].wait_recv()
+    split_r(STEPS + 1, qf[0])
+    p_of[3].wait_recv()
+    split_r(STEPS + 3, qf[2])
+    lax.fori_loop(SERVED * CAP, PIECES * CAP, one_piece, 0)
     local = [
         pltpu.make_async_copy(outs.at[PIECES - 2 + n], in_ref.at[c], l_sem.at[n])
         for n, c in enumerate((gy, opposite))

time: 112 us -> 112 us (level)
  no operation moved by 1% of the time
where the time goes in v6:
time: 112 us
  Pallas kernels  112 us (100%)
    pallas_call x1, Pallas kernels, exchange(): pl.pallas_call(exchange_kernel, out_shape=(jax.ShapeDtypeStruct((PLANE, C...  106 us
    pallas_call x1, Pallas kernels, assemble(): pl.pallas_call(assemble_kernel, out_shape=jax.ShapeDtypeStruct((slots, TI...  5.51 us

profile of v6, /device:TPU:1, one launch (start us, length us, event | category | flops | bytes accessed | tf_op | source)
XLA Modules:
  0.0 112.0 jit_solution(7526578048453088244)
XLA Ops:
  0.0 106.4 %exchange.1 = (f32[16,3,2,128,128]{4,3,2,1,0:T(8,128)}, s32[17]{0:T(128)}) custom-call(s32[2080]{0:T(1024)} %owner_any.1, s32[2080]{0:T(1024)} %owner_any.1, s32[2080]{0:T(1024)} %slot_any.1, s32[2080]{0:T(1024)} %constant.2.clone.code_any, f32[128,1024]{1,0:T(8,128)} %a_any.1), custom_call_target="tpu_custom_call" | custom-call | tf_op jit(solution)/shard_map/exchange/pallas_call | solution.py:455
  106.4 5.5 %assemble.1 = f32[17,256,256]{2,1,0:T(8,128)} custom-call(s32[17]{0:T(128)} %get-tuple-element.7.table, f32[16,3,2,128,128]{4,3,2,1,0:T(8,128)} %get-tuple-element.8.in_ref), custom_call_target="tpu_custom_call" | custom-call | tf_op jit(solution)/shard_map/assemble/pallas_call | solution.py:542

commit v7 on v6

--- a/solution.py
+++ b/solution.py
@@ -72,7 +72,6 @@
 
     ahead = (gx + 2) % GROUPS
     behind = (gx + 6) % GROUPS
-    beyond = (gx + 4) % GROUPS
     partner = gx + 1 - 2 * core
 
     loads = [
@@ -89,10 +88,10 @@
         pl.semaphore_signal(
             barrier, inc=1, device_id={"gx": gx, "gy": at(du, dv)}, device_id_type=MESH
         )
-    for other in (ahead, behind, beyond, partner):
+    for other in (ahead, behind, partner):
         pl.semaphore_signal(barrier, inc=1, device_id={"gx": other, "gy": gy}, device_id_type=MESH)
     loads[0].wait()
-    pl.semaphore_wait(barrier, 8)
+    pl.semaphore_wait(barrier, 7)
 
     def rows_of(c, h, size):
         return pl.ds(pl.multiple_of(c % 2 * CHUNK + h * HALF, HALF), size)
@@ -102,6 +101,9 @@
 
     def whole(c):
         return g.at[c // 2, rows_of(c, 0, CHUNK)]
+
+    def part(ref, n, h):
+        return ref.at[n, pl.ds(h * HALF, HALF)]
 
     def own_half(h):
         return a_ref.at[pl.ds(h * HALF, HALF)]
@@ -150,14 +152,14 @@
         return remote(src, dst, z_send.at[n], z_recv.at[n], to, gy)
 
     z_near = along_z(0, a_ref, rf.at[1], ahead)
-    z_far = along_z(1, a_ref, rf.at[3], beyond)
+    z_far = along_z(1, rf.at[1], rf.at[3], ahead)
 
     def along_q(n, src, dst, to):
         return remote(src, dst, q_send.at[n], q_recv.at[n], to, gy)
 
     opposite = at(2, 2)
-    q_near = along_q(0, whole(opposite), qf.at[1], ahead)
-    q_far = along_q(1, whole(opposite), qf.at[3], beyond)
+    q_near = [along_q(h, half(opposite, h), part(qf, 1, h), ahead) for h in (0, 1)]
+    q_far = [along_q(2 + h, part(qf, 1, h), part(qf, 3, h), ahead) for h in (0, 1)]
 
     def to_partner(n, src, dst):
         return remote(src, dst, p_send.at[n], p_recv.at[n], partner, gy)
@@ -171,7 +173,6 @@
         for d in (0, 1):
             start(b1[0][d][p])
     start(z_near)
-    start(z_far)
 
     @pl.when(core == 0)
     def _():
@@ -280,23 +281,24 @@
         start(a2[d])
     for d in (0, 1):
         a1[d][1].wait_recv()
-    for p in (0, 1):
-        for d in (0, 1):
-            start(b1[1][d][p])
+    for d in (0, 1):
+        start(b1[1][d][0])
     for d in (0, 1):
         split_g(at(-1 + 2 * d, 0))
     for d in (0, 1):
         a2[d].wait_recv()
         start(b1[3][d][0])
     for d in (0, 1):
-        start(b1[3][d][1])
-    for d in (0, 1):
         b1[0][d][0].wait_recv()
         start(b2[0][d])
+    for d in (0, 1):
+        start(b1[3][d][1])
     split_g(at(2, 0))
     for d in (0, 1):
         b1[3][d][0].wait_recv()
         start(b2[3][d])
+    for d in (0, 1):
+        start(b1[1][d][1])
     for p in (0, 1):
         for d in (0, 1):
             start(b1[2][d][p])
@@ -304,6 +306,7 @@
         b1[1][d][0].wait_recv()
         start(b2[1][d])
     z_near.wait_recv()
+    start(z_far)
 
     @pl.when(core == 0)
     def _():
@@ -325,8 +328,8 @@
     take_far(0)
     for d in (0, 1):
         b2[3][d].wait_recv()
-    start(q_near)
-    start(q_far)
+    for h in (0, 1):
+        start(q_near[h])
 
     @pl.when(core == 0)
     def _():
@@ -349,6 +352,8 @@
     lax.fori_loop(0, slots, count, 0)
     take_v(2)
     take_far(1)
+    q_near[0].wait_recv()
+    start(q_far[0])
     take_far(2)
 
     row_in = lax.broadcasted_iota(jnp.int32, (CHUNK, TILE), 0)
@@ -385,7 +390,8 @@
         return carry
 
     lax.fori_loop(0, SERVED, one_piece, 0)
-    q_near.wait_recv()
+    q_near[1].wait_recv()
+    start(q_far[1])
 
     @pl.when(core == 0)
     def _():
@@ -397,7 +403,8 @@
 
     split_r(STEPS + 2, qf[1])
     lax.fori_loop(SERVED, SERVED * CAP, one_piece, 0)
-    q_far.wait_recv()
+    for h in (0, 1):
+        q_far[h].wait_recv()
 
     @pl.when(core == 1)
     def _():
@@ -479,7 +486,7 @@
             pltpu.SMEM((slots,), jnp.int32),
             dma((2, 2)), dma((2, 2)), dma((2,)), dma((2,)),
             dma((4, 2, 2)), dma((4, 2, 2)), dma((4, 2)), dma((4, 2)),
-            dma((2,)), dma((2,)), dma((4,)), dma((4,)), dma((2,)), dma((2,)),
+            dma((2,)), dma((2,)), dma((4,)), dma((4,)), dma((4,)), dma((4,)),
             dma((PIECES, CAP)), dma((PLANE, CAP)), dma((4,)),
         ],
         compiler_params=pltpu.CompilerParams(

time: 112 us -> 110 us (0.982)
  Pallas kernels: 112 us -> 110 us
    pallas_call x1, Pallas kernels: 106 us -> 104 us  [exchange(): pl.pallas_call(exchange_kernel, out_shape=(jax.ShapeDtypeStruct((PLANE, C...]
where the time goes in v7:
time: 110 us
  Pallas kernels  110 us (100%)
    pallas_call x1, Pallas kernels, exchange(): pl.pallas_call(exchange_kernel, out_shape=(jax.ShapeDtypeStruct((PLANE, C...  104 us
    pallas_call x1, Pallas kernels, assemble(): pl.pallas_call(assemble_kernel, out_shape=jax.ShapeDtypeStruct((slots, TI...  5.51 us

profile of v7, /device:TPU:1, one launch (start us, length us, event | category | flops | bytes accessed | tf_op | source)
XLA Modules:
  0.0 109.6 jit_solution(6704732132632773856)
XLA Ops:
  0.0 104.1 %exchange.1 = (f32[16,3,2,128,128]{4,3,2,1,0:T(8,128)}, s32[17]{0:T(128)}) custom-call(s32[2080]{0:T(1024)} %owner_any.1, s32[2080]{0:T(1024)} %owner_any.1, s32[2080]{0:T(1024)} %slot_any.1, s32[2080]{0:T(1024)} %constant.2.clone.code_any, f32[128,1024]{1,0:T(8,128)} %a_any.1), custom_call_target="tpu_custom_call" | custom-call | tf_op jit(solution)/shard_map/exchange/pallas_call | solution.py:462
  104.1 5.5 %assemble.1 = f32[17,256,256]{2,1,0:T(8,128)} custom-call(s32[17]{0:T(128)} %get-tuple-element.7.table, f32[16,3,2,128,128]{4,3,2,1,0:T(8,128)} %get-tuple-element.8.in_ref), custom_call_target="tpu_custom_call" | custom-call | tf_op jit(solution)/shard_map/assemble/pallas_call | solution.py:549

commit v8 on v7

--- a/solution.py
+++ b/solution.py
@@ -457,7 +457,7 @@
     lower_i, lower_j = np.tril_indices(TILE_COUNT)
     code = jnp.asarray(lower_i * TILE_COUNT + lower_j, jnp.int32)
     smem = pl.BlockSpec(memory_space=pltpu.SMEM)
-    hbm = pl.BlockSpec(memory_space=pl.ANY)
+    hbm = pl.BlockSpec(memory_space=pltpu.HBM)
     dma = pltpu.SemaphoreType.DMA
     return pl.pallas_call(
         exchange_kernel,
@@ -466,7 +466,7 @@
             jax.ShapeDtypeStruct((slots,), jnp.int32),
         ),
         in_specs=[smem, hbm, hbm, hbm, hbm],
-        out_specs=(hbm, smem),
+        out_specs=(pl.BlockSpec(memory_space=pltpu.VMEM), smem),
         scratch_shapes=[
             pltpu.VMEM((rows, width), jnp.float32),
             pltpu.VMEM((count,), jnp.int32),
@@ -490,56 +490,56 @@
             dma((PIECES, CAP)), dma((PLANE, CAP)), dma((4,)),
         ],
         compiler_params=pltpu.CompilerParams(
-            collective_id=0, has_side_effects=True, vmem_limit_bytes=56 * 1024 * 1024
+            collective_id=0, has_side_effects=True, vmem_limit_bytes=42 * 1024 * 1024
         ),
         name="exchange",
-    )(tile_owner, tile_owner, tile_slot, code, matrix_rows)
-
-
-def assemble_kernel(table, in_ref, out_ref, tiles, in_sem, out_sem):
-    slots = tiles.shape[0]
-
-    def pieces(q, act):
+    )(tile_owner, *(pltpu.with_memory_space_constraint(x, pltpu.HBM) for x in (tile_owner, tile_slot, code, matrix_rows)))
+
+
+def assemble_kernel(table, in_ref, out_ref, blank, out_sem):
+    slots = table.shape[0]
+
+    def quarters(q, act):
         entry = table[q]
         across = entry % 4 == 1
         source = entry // 4 % HALF_TILES * 2
-        rank = entry // 32
         for h in range(2):
             for c in range(2):
                 row = pl.multiple_of(jnp.where(across, h, c) * CHUNK, CHUNK)
                 col = pl.multiple_of(jnp.where(across, c, h) * CHUNK, CHUNK)
-                act(pltpu.make_async_copy(
-                    in_ref.at[source + h, rank, c],
-                    tiles.at[q, pl.ds(row, CHUNK), pl.ds(col, CHUNK)],
-                    in_sem.at[q, 2 * h + c],
-                ))
-
-    def fetch(q, carry):
+                place = out_ref.at[q, pl.ds(row, CHUNK), pl.ds(col, CHUNK)]
+                act(pltpu.make_async_copy(in_ref.at[source + h, entry // 32, c], place, out_sem.at[q, 2 * h + c]))
+
+    def clear(q):
+        return pltpu.make_async_copy(blank, out_ref.at[q], out_sem.at[q, 0])
+
+    def put(q, carry):
         present = table[q] % 4 > 0
 
         @pl.when(present)
         def _():
-            pieces(q, lambda copy: copy.start())
+            quarters(q, lambda copy: copy.start())
 
         @pl.when(jnp.logical_not(present))
         def _():
-            tiles[q] = jnp.zeros((TILE, TILE), jnp.float32)
-
-        return carry
-
-    def put(q, carry):
-        @pl.when(table[q] % 4 > 0)
+            blank[...] = jnp.zeros(blank.shape, jnp.float32)
+            clear(q).start()
+
+        return carry
+
+    def finish(q, carry):
+        present = table[q] % 4 > 0
+
+        @pl.when(present)
         def _():
-            pieces(q, lambda copy: copy.wait())
-
-        pltpu.make_async_copy(tiles.at[q], out_ref.at[q], out_sem.at[q]).start()
-        return carry
-
-    def finish(q, carry):
-        pltpu.make_async_copy(tiles.at[q], out_ref.at[q], out_sem.at[q]).wait()
-        return carry
-
-    lax.fori_loop(0, slots, fetch, 0)
+            quarters(q, lambda copy: copy.wait())
+
+        @pl.when(jnp.logical_not(present))
+        def _():
+            clear(q).wait()
+
+        return carry
+
     lax.fori_loop(0, slots, put, 0)
     lax.fori_loop(0, slots, finish, 0)
 
@@ -549,13 +549,13 @@
     return pl.pallas_call(
         assemble_kernel,
         out_shape=jax.ShapeDtypeStruct((slots, TILE, TILE), jnp.float32),
-        in_specs=[pl.BlockSpec(memory_space=pltpu.SMEM), pl.BlockSpec(memory_space=pl.ANY)],
+        in_specs=[pl.BlockSpec(memory_space=pltpu.SMEM), pl.BlockSpec(memory_space=pltpu.VMEM)],
         out_specs=pl.BlockSpec(memory_space=pl.ANY),
         scratch_shapes=[
-            pltpu.VMEM((slots, TILE, TILE), jnp.float32),
+            pltpu.VMEM((TILE, TILE), jnp.float32),
             pltpu.SemaphoreType.DMA((slots, 4)),
-            pltpu.SemaphoreType.DMA((slots,)),
         ],
+        compiler_params=pltpu.CompilerParams(vmem_limit_bytes=16 * 1024 * 1024),
         name="assemble",
     )(table, incoming)
 

time: 110 us -> 108 us (0.982)
  Pallas kernels: 110 us -> 107 us
    pallas_call x1, Pallas kernels: 5.51 us -> 3.23 us  [assemble(): pl.pallas_call(assemble_kernel, out_shape=jax.ShapeDtypeStruct((slots, TI...]
where the time goes in v8:
time: 108 us; the launch traced here: 107 us
  Pallas kernels  107 us (99%)
    pallas_call x1, Pallas kernels, exchange(): pl.pallas_call(exchange_kernel, out_shape=(jax.ShapeDtypeStruct((PLANE, C...  104 us
    pallas_call x1, Pallas kernels, assemble(): pl.pallas_call(assemble_kernel, out_shape=jax.ShapeDtypeStruct((slots, TI...  3.23 us

profile of v8, /device:TPU:1, one launch (start us, length us, event | category | flops | bytes accessed | tf_op | source)
XLA Modules:
  0.0 107.4 jit_solution(6903892862469755142)
XLA Ops:
  0.0 104.2 %exchange.1 = (f32[16,3,2,128,128]{4,3,2,1,0:T(8,128)S(1)}, s32[17]{0:T(128)S(1)}) custom-call(s32[2080]{0:T(1024)} %owner_any.1, s32[2080]{0:T(1024)} %owner_any.1, s32[2080]{0:T(1024)} %slot_any.1, s32[2080]{0:T(1024)} %constant.2.clone.code_any, f32[128,1024]{1,0:T(8,128)} %a_any.1), custom_call_target="tpu_custom_call" | custom-call | tf_op jit(solution)/shard_map/exchange/pallas_call | solution.py:462
  104.2 3.2 %assemble.1 = f32[17,256,256]{2,1,0:T(8,128)} custom-call(s32[17]{0:T(128)S(1)} %get-tuple-element.7.table, f32[16,3,2,128,128]{4,3,2,1,0:T(8,128)S(1)} %get-tuple-element.8.in_ref), custom_call_target="tpu_custom_call" | custom-call | tf_op jit(solution)/shard_map/assemble/pallas_call | solution.py:549

commit v9 on v8

--- a/solution.py
+++ b/solution.py
@@ -21,6 +21,7 @@
 ORDER = ((2, 0), (0, 1), (1, 9), (0, 3), (3, 9), (1, 0), (3, 0), (0, 0))
 SERVED = len(ORDER)
 PIECES = 2 * SERVED
+LEAVING = SERVED - 1
 
 
 def entry_of(e, gx, r):
@@ -363,8 +364,10 @@
         return lax.dot_general(p, q, (((1,), (1,)), ((), ())), preferred_element_type=jnp.float32)
 
     def one_piece(i, carry):
-        k = i // SERVED % CAP
-        p = i % SERVED * 2 + i // (SERVED * CAP)
+        away = i < 2 * LEAVING * CAP
+        n = jnp.where(away, i % LEAVING, LEAVING)
+        k = jnp.where(away, i // LEAVING % CAP, i % CAP)
+        p = n * 2 + jnp.where(away, i // (LEAVING * CAP), (i - 2 * LEAVING * CAP) // CAP)
         to = served(p // 2, p % 2)
         chunk = jnp.where(p % 2 == 0, gy, opposite)
         entry = send_tab[p * CAP + k]
@@ -381,15 +384,13 @@
             part = value[:, c * CHUNK:(c + 1) * CHUNK]
             outs[p, k, c] = jnp.where(rowwise, part, part.T)
 
-        @pl.when(p < PIECES - 2)
+        @pl.when(away)
         def _():
-            remote(
-                outs.at[p, k], in_ref.at[chunk, k], x_send.at[p, k], x_recv.at[chunk, k], gx, to
-            ).start()
+            remote(outs.at[p, k], in_ref.at[chunk, k], x_send, x_recv, gx, to).start()
 
         return carry
 
-    lax.fori_loop(0, SERVED, one_piece, 0)
+    lax.fori_loop(0, LEAVING, one_piece, 0)
     q_near[1].wait_recv()
     start(q_far[1])
 
@@ -402,7 +403,7 @@
         to_partner(2, qf.at[1], qf.at[0]).start()
 
     split_r(STEPS + 2, qf[1])
-    lax.fori_loop(SERVED, SERVED * CAP, one_piece, 0)
+    lax.fori_loop(LEAVING, LEAVING * CAP, one_piece, 0)
     for h in (0, 1):
         q_far[h].wait_recv()
 
@@ -415,7 +416,7 @@
     split_r(STEPS + 1, qf[0])
     p_of[3].wait_recv()
     split_r(STEPS + 3, qf[2])
-    lax.fori_loop(SERVED * CAP, PIECES * CAP, one_piece, 0)
+    lax.fori_loop(LEAVING * CAP, PIECES * CAP, one_piece, 0)
     local = [
         pltpu.make_async_copy(outs.at[PIECES - 2 + n], in_ref.at[c], l_sem.at[n])
         for n, c in enumerate((gy, opposite))
@@ -427,28 +428,9 @@
     for copy in local:
         copy.wait()
 
-    def sent(i, carry):
-        remote(
-            outs.at[i // CAP, i % CAP], in_ref.at[0, 0], x_send.at[i // CAP, i % CAP], x_recv.at[0, 0], ahead, gy
-        ).wait_send()
-        return carry
-
-    lax.fori_loop(0, (PIECES - 2) * CAP, sent, 0)
-
-    def arrived(i, carry):
-        du = i // CAP // SIDE
-        dv = i // CAP % SIDE
-        chunk = at(du, dv)
-
-        @pl.when(jnp.logical_or(du != dv, du % 2 > 0))
-        def _():
-            remote(
-                outs.at[0, 0], in_ref.at[chunk, i % CAP], x_send.at[0, 0], x_recv.at[chunk, i % CAP], ahead, gy
-            ).wait_recv()
-
-        return carry
-
-    lax.fori_loop(0, PLANE * CAP, arrived, 0)
+    everything = remote(outs.at[pl.ds(0, 2 * LEAVING)], in_ref.at[pl.ds(0, 2 * LEAVING)], x_send, x_recv, ahead, gy)
+    everything.wait_send()
+    everything.wait_recv()
 
 
 def exchange(matrix_rows, tile_owner, tile_slot, slots):
@@ -487,7 +469,7 @@
             dma((2, 2)), dma((2, 2)), dma((2,)), dma((2,)),
             dma((4, 2, 2)), dma((4, 2, 2)), dma((4, 2)), dma((4, 2)),
             dma((2,)), dma((2,)), dma((4,)), dma((4,)), dma((4,)), dma((4,)),
-            dma((PIECES, CAP)), dma((PLANE, CAP)), dma((4,)),
+            dma(()), dma(()), dma((4,)),
         ],
         compiler_params=pltpu.CompilerParams(
             collective_id=0, has_side_effects=True, vmem_limit_bytes=42 * 1024 * 1024

time: 108 us -> 105 us (0.972)
  Pallas kernels: 107 us -> 104 us
    pallas_call x1, Pallas kernels: 104 us -> 101 us  [exchange(): pl.pallas_call(exchange_kernel, out_shape=(jax.ShapeDtypeStruct((PLANE, C...]
where the time goes in v9:
time: 105 us; the launch traced here: 104 us
  Pallas kernels  104 us (99%)
    pallas_call x1, Pallas kernels, exchange(): pl.pallas_call(exchange_kernel, out_shape=(jax.ShapeDtypeStruct((PLANE, C...  101 us
    pallas_call x1, Pallas kernels, assemble(): pl.pallas_call(assemble_kernel, out_shape=jax.ShapeDtypeStruct((slots, TI...  3.23 us

profile of v9, /device:TPU:1, one launch (start us, length us, event | category | flops | bytes accessed | tf_op | source)
XLA Modules:
  0.0 104.4 jit_solution(15237197023065575780)
XLA Ops:
  0.0 101.1 %exchange.1 = (f32[16,3,2,128,128]{4,3,2,1,0:T(8,128)S(1)}, s32[17]{0:T(128)S(1)}) custom-call(s32[2080]{0:T(1024)} %owner_any.1, s32[2080]{0:T(1024)} %owner_any.1, s32[2080]{0:T(1024)} %slot_any.1, s32[2080]{0:T(1024)} %constant.2.clone.code_any, f32[128,1024]{1,0:T(8,128)} %a_any.1), custom_call_target="tpu_custom_call" | custom-call | tf_op jit(solution)/shard_map/exchange/pallas_call | solution.py:444
  101.1 3.2 %assemble.1 = f32[17,256,256]{2,1,0:T(8,128)} custom-call(s32[17]{0:T(128)S(1)} %get-tuple-element.7.table, f32[16,3,2,128,128]{4,3,2,1,0:T(8,128)S(1)} %get-tuple-element.8.in_ref), custom_call_target="tpu_custom_call" | custom-call | tf_op jit(solution)/shard_map/assemble/pallas_call | solution.py:531

commit v10 on v9

--- a/solution.py
+++ b/solution.py
@@ -54,7 +54,7 @@
 def exchange_kernel(
     owner_smem, owner_any, slot_any, code_any, a_any, in_ref, table_ref,
     a_ref, owner_ref, slot_ref, code_ref,
-    g, ghi, glo, rf, qf, rhi, rlo, outs, target_tab, entry_tab, send_tab, found_tab,
+    g, ghi, glo, rf, qf, rows_ref, outs, target_tab, entry_tab, send_tab, found_tab,
     a1_send, a1_recv, a2_send, a2_recv, b1_send, b1_recv, b2_send, b2_recv,
     z_send, z_recv, p_send, p_recv, q_send, q_recv, x_send, x_recv, l_sem,
 ):
@@ -81,9 +81,6 @@
             ((a_any, a_ref), (owner_any, owner_ref), (slot_any, slot_ref), (code_any, code_ref))
         )
     ]
-    for load in loads:
-        load.start()
-
     barrier = pltpu.get_barrier_semaphore()
     for du, dv in ((1, 0), (3, 0), (0, 1), (0, 3)):
         pl.semaphore_signal(
@@ -91,6 +88,8 @@
         )
     for other in (ahead, behind, partner):
         pl.semaphore_signal(barrier, inc=1, device_id={"gx": other, "gy": gy}, device_id_type=MESH)
+    for load in loads:
+        load.start()
     loads[0].wait()
     pl.semaphore_wait(barrier, 7)
 
@@ -192,8 +191,8 @@
 
     def split_r(n, value):
         high, low = split(value)
-        rhi[n] = high
-        rlo[n] = low
+        rows_ref[n, :CHUNK] = high
+        rows_ref[n, CHUNK:] = low
 
     for cls, chunk in enumerate((gy, opposite)):
         class_r = chunk // 2
@@ -229,8 +228,8 @@
     lax.fori_loop(0, PIECES, fill, 0)
     split_r(0, a_ref[...])
     block, rows = me // 2, rows_of(me, 0, CHUNK)
-    ghi[block, rows, :] = rhi[0]
-    glo[block, rows, :] = rlo[0]
+    ghi[block, rows, :] = rows_ref[0, :CHUNK]
+    glo[block, rows, :] = rows_ref[0, CHUNK:]
 
     for load in loads[1:]:
         load.wait()
@@ -285,27 +284,25 @@
     for d in (0, 1):
         start(b1[1][d][0])
     for d in (0, 1):
-        split_g(at(-1 + 2 * d, 0))
-    for d in (0, 1):
         a2[d].wait_recv()
         start(b1[3][d][0])
     for d in (0, 1):
         b1[0][d][0].wait_recv()
         start(b2[0][d])
     for d in (0, 1):
-        start(b1[3][d][1])
+        start(b1[2][d][0])
+    for d in (0, 1):
+        split_g(at(-1 + 2 * d, 0))
     split_g(at(2, 0))
     for d in (0, 1):
         b1[3][d][0].wait_recv()
         start(b2[3][d])
     for d in (0, 1):
-        start(b1[1][d][1])
-    for p in (0, 1):
-        for d in (0, 1):
-            start(b1[2][d][p])
-    for d in (0, 1):
         b1[1][d][0].wait_recv()
         start(b2[1][d])
+    for n in (3, 1, 2):
+        for d in (0, 1):
+            start(b1[n][d][1])
     z_near.wait_recv()
     start(z_far)
 
@@ -340,9 +337,7 @@
         b1[2][d][0].wait_recv()
         start(b2[2][d])
     split_g(opposite)
-    high, low = split(whole(opposite)[...])
-    rhi[STEPS] = high
-    rlo[STEPS] = low
+    split_r(STEPS, whole(opposite)[...])
     lax.fori_loop(0, slots, find, 0)
     take_v(1)
     take_v(3)
@@ -373,9 +368,8 @@
         entry = send_tab[p * CAP + k]
         s = entry // 32
         j = entry // 4 % HALF_TILES
-        rh = rhi[s]
-        gh = ghi[j]
-        value = dot(rh, gh) + dot(rh, glo[j]) + dot(rlo[s], gh)
+        both = dot(rows_ref[s], ghi[j])
+        value = both[:CHUNK] + both[CHUNK:] + dot(rows_ref[s, :CHUNK], glo[j])
         upper = row_in + chunk % 2 * CHUNK < col_in
         masked = jnp.logical_and(upper, entry // 2 % 2 > 0)
         value = jnp.where(masked, jnp.float32(0.0), value)
@@ -459,8 +453,7 @@
             pltpu.VMEM((HALF_TILES, TILE, width), jnp.bfloat16),
             pltpu.VMEM((4, CHUNK, width), jnp.float32),
             pltpu.VMEM((4, CHUNK, width), jnp.float32),
-            pltpu.VMEM((2 * STEPS, CHUNK, width), jnp.bfloat16),
-            pltpu.VMEM((2 * STEPS, CHUNK, width), jnp.bfloat16),
+            pltpu.VMEM((2 * STEPS, 2 * CHUNK, width), jnp.bfloat16),
             pltpu.VMEM((PIECES, CAP, 2, CHUNK, CHUNK), jnp.float32),
             pltpu.SMEM((2 * ENTRIES,), jnp.int32),
             pltpu.SMEM((2 * ENTRIES,), jnp.int32),

time: 105 us -> 103 us (0.981)
    pallas_call x1, Pallas kernels: 101 us -> 100 us  [exchange(): pl.pallas_call(exchange_kernel, out_shape=(jax.ShapeDtypeStruct((PLANE, C...]
where the time goes in v10:
time: 103 us
  Pallas kernels  103 us (100%)
    pallas_call x1, Pallas kernels, exchange(): pl.pallas_call(exchange_kernel, out_shape=(jax.ShapeDtypeStruct((PLANE, C...  100 us
    pallas_call x1, Pallas kernels, assemble(): pl.pallas_call(assemble_kernel, out_shape=jax.ShapeDtypeStruct((slots, TI...  3.23 us

profile of v10, /device:TPU:1, one launch (start us, length us, event | category | flops | bytes accessed | tf_op | source)
XLA Modules:
  0.0 103.3 jit_solution(9798032618009006032)
XLA Ops:
  0.0 100.0 %exchange.1 = (f32[16,3,2,128,128]{4,3,2,1,0:T(8,128)S(1)}, s32[17]{0:T(128)S(1)}) custom-call(s32[2080]{0:T(1024)} %owner_any.1, s32[2080]{0:T(1024)} %owner_any.1, s32[2080]{0:T(1024)} %slot_any.1, s32[2080]{0:T(1024)} %constant.2.clone.code_any, f32[128,1024]{1,0:T(8,128)} %a_any.1), custom_call_target="tpu_custom_call" | custom-call | tf_op jit(solution)/shard_map/exchange/pallas_call | solution.py:438
  100.0 3.2 %assemble.1 = f32[17,256,256]{2,1,0:T(8,128)} custom-call(s32[17]{0:T(128)S(1)} %get-tuple-element.7.table, f32[16,3,2,128,128]{4,3,2,1,0:T(8,128)S(1)} %get-tuple-element.8.in_ref), custom_call_target="tpu_custom_call" | custom-call | tf_op jit(solution)/shard_map/assemble/pallas_call | solution.py:524

commit v11 on v10

--- a/solution.py
+++ b/solution.py
@@ -483,7 +483,7 @@
                 row = pl.multiple_of(jnp.where(across, h, c) * CHUNK, CHUNK)
                 col = pl.multiple_of(jnp.where(across, c, h) * CHUNK, CHUNK)
                 place = out_ref.at[q, pl.ds(row, CHUNK), pl.ds(col, CHUNK)]
-                act(pltpu.make_async_copy(in_ref.at[source + h, entry // 32, c], place, out_sem.at[q, 2 * h + c]))
+                act(pltpu.make_async_copy(in_ref.at[source + h, entry // 32, c], place, out_sem.at[q, 2 * h + c]), h)
 
     def clear(q):
         return pltpu.make_async_copy(blank, out_ref.at[q], out_sem.at[q, 0])
@@ -493,7 +493,7 @@
 
         @pl.when(present)
         def _():
-            quarters(q, lambda copy: copy.start())
+            quarters(q, lambda copy, thread: copy.start(priority=thread))
 
         @pl.when(jnp.logical_not(present))
         def _():
@@ -507,7 +507,7 @@
 
         @pl.when(present)
         def _():
-            quarters(q, lambda copy: copy.wait())
+            quarters(q, lambda copy, thread: copy.wait())
 
         @pl.when(jnp.logical_not(present))
         def _():

time: 103 us -> 103 us (level)
  no operation moved by 1% of the time
where the time goes in v11:
time: 103 us
  Pallas kernels  103 us (100%)
    pallas_call x1, Pallas kernels, exchange(): pl.pallas_call(exchange_kernel, out_shape=(jax.ShapeDtypeStruct((PLANE, C...  100 us
    pallas_call x1, Pallas kernels, assemble(): pl.pallas_call(assemble_kernel, out_shape=jax.ShapeDtypeStruct((slots, TI...  3.21 us

profile of v11, /device:TPU:1, one launch (start us, length us, event | category | flops | bytes accessed | tf_op | source)
XLA Modules:
  0.0 103.2 jit_solution(2019954913563506583)
XLA Ops:
  0.0 100.0 %exchange.1 = (f32[16,3,2,128,128]{4,3,2,1,0:T(8,128)S(1)}, s32[17]{0:T(128)S(1)}) custom-call(s32[2080]{0:T(1024)} %owner_any.1, s32[2080]{0:T(1024)} %owner_any.1, s32[2080]{0:T(1024)} %slot_any.1, s32[2080]{0:T(1024)} %constant.2.clone.code_any, f32[128,1024]{1,0:T(8,128)} %a_any.1), custom_call_target="tpu_custom_call" | custom-call | tf_op jit(solution)/shard_map/exchange/pallas_call | solution.py:438
  100.0 3.2 %assemble.1 = f32[17,256,256]{2,1,0:T(8,128)} custom-call(s32[17]{0:T(128)S(1)} %get-tuple-element.7.table, f32[16,3,2,128,128]{4,3,2,1,0:T(8,128)S(1)} %get-tuple-element.8.in_ref), custom_call_target="tpu_custom_call" | custom-call | tf_op jit(solution)/shard_map/assemble/pallas_call | solution.py:524

commit v12 on v10

--- a/solution.py
+++ b/solution.py
@@ -483,10 +483,10 @@
                 row = pl.multiple_of(jnp.where(across, h, c) * CHUNK, CHUNK)
                 col = pl.multiple_of(jnp.where(across, c, h) * CHUNK, CHUNK)
                 place = out_ref.at[q, pl.ds(row, CHUNK), pl.ds(col, CHUNK)]
-                act(pltpu.make_async_copy(in_ref.at[source + h, entry // 32, c], place, out_sem.at[q, 2 * h + c]))
+                act(pltpu.make_async_copy(in_ref.at[source + h, entry // 32, c], place, out_sem))
 
     def clear(q):
-        return pltpu.make_async_copy(blank, out_ref.at[q], out_sem.at[q, 0])
+        return pltpu.make_async_copy(blank, out_ref.at[q], out_sem)
 
     def put(q, carry):
         present = table[q] % 4 > 0
@@ -502,21 +502,8 @@
 
         return carry
 
-    def finish(q, carry):
-        present = table[q] % 4 > 0
-
-        @pl.when(present)
-        def _():
-            quarters(q, lambda copy: copy.wait())
-
-        @pl.when(jnp.logical_not(present))
-        def _():
-            clear(q).wait()
-
-        return carry
-
     lax.fori_loop(0, slots, put, 0)
-    lax.fori_loop(0, slots, finish, 0)
+    pltpu.make_async_copy(out_ref, out_ref, out_sem).wait()
 
 
 def assemble(table, incoming):
@@ -528,7 +515,7 @@
         out_specs=pl.BlockSpec(memory_space=pl.ANY),
         scratch_shapes=[
             pltpu.VMEM((TILE, TILE), jnp.float32),
-            pltpu.SemaphoreType.DMA((slots, 4)),
+            pltpu.SemaphoreType.DMA(()),
         ],
         compiler_params=pltpu.CompilerParams(vmem_limit_bytes=16 * 1024 * 1024),
         name="assemble",

time: 103 us -> 103 us (level)
  no operation moved by 1% of the time
where the time goes in v12:
time: 103 us
  Pallas kernels  103 us (100%)
    pallas_call x1, Pallas kernels, exchange(): pl.pallas_call(exchange_kernel, out_shape=(jax.ShapeDtypeStruct((PLANE, C...  100 us
    pallas_call x1, Pallas kernels, assemble(): pl.pallas_call(assemble_kernel, out_shape=jax.ShapeDtypeStruct((slots, TI...  2.61 us

profile of v12, /device:TPU:1, one launch (start us, length us, event | category | flops | bytes accessed | tf_op | source)
XLA Modules:
  0.0 102.6 jit_solution(13698254849178901915)
XLA Ops:
  0.0 100.0 %exchange.1 = (f32[16,3,2,128,128]{4,3,2,1,0:T(8,128)S(1)}, s32[17]{0:T(128)S(1)}) custom-call(s32[2080]{0:T(1024)} %owner_any.1, s32[2080]{0:T(1024)} %owner_any.1, s32[2080]{0:T(1024)} %slot_any.1, s32[2080]{0:T(1024)} %constant.2.clone.code_any, f32[128,1024]{1,0:T(8,128)} %a_any.1), custom_call_target="tpu_custom_call" | custom-call | tf_op jit(solution)/shard_map/exchange/pallas_call | solution.py:438
  100.0 2.6 %assemble.1 = f32[17,256,256]{2,1,0:T(8,128)} custom-call(s32[17]{0:T(128)S(1)} %get-tuple-element.7.table, f32[16,3,2,128,128]{4,3,2,1,0:T(8,128)S(1)} %get-tuple-element.8.in_ref), custom_call_target="tpu_custom_call" | custom-call | tf_op jit(solution)/shard_map/assemble/pallas_call | solution.py:511
